TPU v7x, 8 devices: a whole 2x2x1 slice. The times are simulated.
8 devices in a mesh: rep: 4 (over z, y, x), fsdp: 2 (over core).
Axes of the slice: x: 2, y: 2, z: 1, core: 2. Of those that a mesh axis runs over, the one named last changes fastest.
Arguments:
- tok_ids: int32 [8, 512], P(('rep', 'fsdp'))
- tok_labels: int32 [8, 512], P(('rep', 'fsdp'))
- tok_pos: int32 [8, 512], P(('rep', 'fsdp'))
- expert_idx: int32 [2, 8, 512, 2], P(None, ('rep', 'fsdp'))
- learn_rate: float32 [], replicated
- embedding: float32 [32064, 512], P('fsdp')
- w_query: float32 [2, 512, 512], P(None, 'fsdp')
- w_key: float32 [2, 512, 128], P(None, 'fsdp')
- w_value: float32 [2, 512, 128], P(None, 'fsdp')
- w_attn_out: float32 [2, 512, 512], P(None, 'fsdp')
- g_attn: float32 [2, 512], P(None, 'fsdp')
- g_mlp: float32 [2, 512], P(None, 'fsdp')
- w_router: float32 [2, 512, 16], P(None, 'fsdp')
- w_gate: float32 [2, 16, 512, 800], P(None, None, 'fsdp')
- w_up: float32 [2, 16, 512, 800], P(None, None, 'fsdp')
- w_down: float32 [2, 16, 800, 512], P(None, None, 'fsdp')
- g_final: float32 [512], P('fsdp')
- w_head: float32 [512, 32064], P('fsdp')
Outputs:
- output 1: float32 [32064, 512], P('fsdp')
- output 2: float32 [2, 512, 512], P(None, 'fsdp')
- output 3: float32 [2, 512, 128], P(None, 'fsdp')
- output 4: float32 [2, 512, 128], P(None, 'fsdp')
- output 5: float32 [2, 512, 512], P(None, 'fsdp')
- output 6: float32 [2, 512], P(None, 'fsdp')
- output 7: float32 [2, 512], P(None, 'fsdp')
- output 8: float32 [2, 512, 16], P(None, 'fsdp')
- output 9: float32 [2, 16, 512, 800], P(None, None, 'fsdp')
- output 10: float32 [2, 16, 512, 800], P(None, None, 'fsdp')
- output 11: float32 [2, 16, 800, 512], P(None, None, 'fsdp')
- output 12: float32 [512], P('fsdp')
- output 13: float32 [512, 32064], P('fsdp')
- output 14: float32 [], replicated
All inputs are finite; a program needn't handle non-finite values.
Results may differ from a plain program's by a relative error of at most 0.00502737.
Values are sent between devices in bfloat16 or wider.
A program may use at most 1.25 GiB of HBM per device.

v0:
```python
import functools
import jax
import jax.numpy as jnp
from jax import lax
from jax.experimental import pallas as pl
from jax.experimental.pallas import tpu as pltpu
from jax.sharding import PartitionSpec as P

HEAD_DIM = 128
ROPE_THETA = 1000000.0
NORM_EPS = 1e-5
LOG2E = 1.4426950408889634
LN2 = 0.6931471805599453
F32 = jnp.float32
BF16 = jnp.bfloat16
I32 = jnp.int32
TILE = 16
HEAD_STEPS = 12
HEAD_PIECE = 512
DW_PIECE = 384
LSE_ROWS = 72
SUBLANES = 8
NEG = -1e30
ROW, COL = 0, 1


def contract(a, b, ca, cb):
    return lax.dot_general(a, b, (((ca,), (cb,)), ((), ())), preferred_element_type=F32)


def dot(a, b):
    return contract(a, b, COL, ROW)


def dot_nt(a, b):
    return contract(a, b, COL, COL)


def dot_tn(a, b):
    return contract(a, b, ROW, ROW)


def get(ref):
    return ref[...]


def put(ref, value):
    ref[...] = value


def fill(ref, value):
    put(ref, jnp.full(ref.shape, value, ref.dtype))


def iota(shape, axis):
    return lax.broadcasted_iota(I32, shape, axis)


def axis_sum(x, axis):
    return jnp.sum(x, axis=axis, keepdims=True)


def keep(mask, x):
    return jnp.where(mask, x, 0.0)


def hot(mask):
    return jnp.where(mask, 1.0, 0.0).astype(BF16)


def pair_of(x, axis):
    return jnp.split(x, 2, axis=axis)


def side_by_side(ref):
    return jnp.concatenate([ref[core].reshape(ref.shape[-2:]) for core in range(2)], axis=COL)


def rms_stats(x):
    return lax.rsqrt(jnp.mean(x * x, axis=-1, keepdims=True) + NORM_EPS)


def rms_norm(x, gain):
    return (x * rms_stats(x) * gain).astype(BF16)


def rms_norm_bwd(x, gain, d_normed):
    inv = rms_stats(x)
    unit = x * inv
    d_gain = axis_sum(d_normed * unit, ROW)
    d_unit = d_normed * gain
    d_x = inv * (d_unit - unit * jnp.mean(d_unit * unit, axis=-1, keepdims=True))
    return d_x, d_gain


def split3(x):
    hi = x.astype(BF16)
    rest = x - hi.astype(F32)
    mid = rest.astype(BF16)
    return hi, mid, (rest - mid.astype(F32)).astype(BF16)


def select_rows(onehot, x):
    hi, mid, lo = split3(x)
    return dot(onehot, hi) + dot(onehot, mid) + dot(onehot, lo)


def params(vmem_mib, **kw):
    return pltpu.CompilerParams(vmem_limit_bytes=vmem_mib << 20, **kw)


def whole(shape):
    zeros = (0,) * len(shape)
    return pl.BlockSpec(shape, lambda *_: zeros)


def route_masks(pos_row, rows):
    return [iota((rows, pos.shape[COL]), ROW) == pos for pos in pair_of(pos_row, ROW)]


def moe_fwd_kernel(off, x_ref, gain_ref, wr_ref, prow_ref, pcol_ref, ecol_ref, wg_ref, wu_ref, wd_ref,
                   out_ref, xs_out, y0_out, y1_out, xs_s, down_s, *, rows, blk):
    expert = pl.program_id(0)
    toks = x_ref.shape[0]

    @pl.when(expert == 0)
    def _():
        normed = rms_norm(get(x_ref), get(gain_ref))
        hit0, hit1 = route_masks(get(prow_ref), rows)
        spread = hot(hit0 | hit1)
        xs = dot(spread, normed).astype(BF16)
        put(xs_out, xs)
        xs_s[pl.ds(0, rows), :] = xs
        xs_s[pl.ds(rows, blk), :] = jnp.zeros((blk, xs.shape[1]), BF16)
        fill(down_s, 0)

    w_gate = side_by_side(wg_ref)
    w_up = side_by_side(wu_ref)
    w_down = get(wd_ref).reshape(w_gate.shape)
    start = off[expert]
    count = off[expert + 1] - start

    def body(i, carry):
        at = pl.multiple_of(start + i * blk, TILE)
        xs = xs_s[pl.ds(at, blk), :]
        gate = dot_nt(w_gate, xs)
        up = dot_nt(w_up, xs)
        hidden = (gate * jax.nn.sigmoid(gate) * up).astype(BF16)
        down_s[pl.ds(at, blk), :] = dot_tn(hidden, w_down)
        return carry

    lax.fori_loop(0, (count + blk - 1) // blk, body, 0)

    @pl.when(expert == pl.num_programs(0) - 1)
    def _():
        x = get(x_ref)
        normed = rms_norm(x, get(gain_ref))
        logits = dot_nt(normed, get(wr_ref))
        gate0, gate1 = pair_gates(logits, get(ecol_ref), COL)
        col_id = iota((toks, rows), COL)
        slot0, slot1 = pair_of(get(pcol_ref), COL)
        pick0 = hot(col_id == slot0)
        pick1 = hot(col_id == slot1)
        hi, mid, lo = split3(down_s[:rows])
        y0 = dot(pick0, hi) + dot(pick0, mid) + dot(pick0, lo)
        y1 = dot(pick1, hi) + dot(pick1, mid) + dot(pick1, lo)
        put(y0_out, y0)
        put(y1_out, y1)
        put(out_ref, x + (y0 * gate0 + y1 * gate1))


def pair_gates(logits, experts, axis):
    ids = iota(logits.shape, axis)
    r0, r1 = [axis_sum(keep(ids == chosen, logits), axis) for chosen in pair_of(experts, axis)]
    top = jnp.maximum(r0, r1)
    e0 = jnp.exp(r0 - top)
    e1 = jnp.exp(r1 - top)
    return e0 / (e0 + e1), e1 / (e0 + e1)


def moe_bwd_kernel(off, dx_ref, x_ref, gain_ref, wr_ref, prow_ref, pcol_ref, erow_ref, ecol_ref, y0_ref, y1_ref, xs_ref,
                   wg_ref, wu_ref, wd_ref, dx_out, dys_out, dwr_out, dg_out, xs_s, dys_s, dxs_s, *, rows, blk):
    expert = pl.program_id(0)
    toks, width = x_ref.shape

    @pl.when(expert == 0)
    def _():
        dx = get(dx_ref)
        normed = rms_norm(get(x_ref), get(gain_ref))
        logits_t = dot_nt(get(wr_ref), normed)
        gate0, gate1 = pair_gates(logits_t, get(erow_ref), ROW)
        hit0, hit1 = route_masks(get(prow_ref), rows)
        spread = hot(hit0 | hit1)
        gate_rows = axis_sum(keep(hit0, gate0) + keep(hit1, gate1), COL)
        dys = select_rows(spread, dx) * gate_rows
        put(dys_out, dys)
        dys_s[pl.ds(0, rows), :] = dys.astype(BF16)
        dys_s[pl.ds(rows, blk), :] = jnp.zeros((blk, width), BF16)
        xs_s[pl.ds(0, rows), :] = get(xs_ref)
        xs_s[pl.ds(rows, blk), :] = jnp.zeros((blk, width), BF16)
        fill(dxs_s, 0)

    w_gate = side_by_side(wg_ref)
    w_up = side_by_side(wu_ref)
    w_down = get(wd_ref).reshape(w_gate.shape)
    start = off[expert]
    count = off[expert + 1] - start

    def body(i, carry):
        at = pl.multiple_of(start + i * blk, TILE)
        xs = xs_s[pl.ds(at, blk), :]
        dys = dys_s[pl.ds(at, blk), :]
        gate = dot_nt(w_gate, xs)
        up = dot_nt(w_up, xs)
        d_hidden = dot_nt(w_down, dys)
        d_gate, d_up, _ = glu_bwd(gate, up, d_hidden)
        dxs_s[pl.ds(at, blk), :] = dot_tn(d_gate, w_gate) + dot_tn(d_up, w_up)
        return carry

    lax.fori_loop(0, (count + blk - 1) // blk, body, 0)

    @pl.when(expert == pl.num_programs(0) - 1)
    def _():
        x = get(x_ref)
        dx = get(dx_ref)
        gain = get(gain_ref)
        normed = rms_norm(x, gain)
        logits = dot_nt(normed, get(wr_ref))
        experts = get(ecol_ref)
        gate0, gate1 = pair_gates(logits, experts, COL)
        d_gate0 = axis_sum(dx * get(y0_ref), COL)
        d_gate1 = axis_sum(dx * get(y1_ref), COL)
        mean = gate0 * d_gate0 + gate1 * d_gate1
        first, second = pair_of(experts, COL)
        ids = iota(logits.shape, COL)
        d_logits = (keep(ids == first, gate0 * (d_gate0 - mean)) + keep(ids == second, gate1 * (d_gate1 - mean))).astype(BF16)
        put(dwr_out, dot_tn(d_logits, normed))
        col_id = iota((toks, rows), COL)
        slot0, slot1 = pair_of(get(pcol_ref), COL)
        collect = hot((col_id == slot0) | (col_id == slot1))
        d_normed = select_rows(collect, dxs_s[pl.ds(0, rows), :]) + dot(d_logits, get(wr_ref))
        d_x, d_gain = rms_norm_bwd(x, gain, d_normed.astype(BF16).astype(F32))
        put(dx_out, dx + d_x)
        put(dg_out, d_gain)


def glu_bwd(gate, up, d_hidden):
    sig = jax.nn.sigmoid(gate)
    act = gate * sig
    d_gate = (d_hidden * up * (sig + act * (1.0 - sig))).astype(BF16)
    d_up = (d_hidden * act).astype(BF16)
    return d_gate, d_up, act


def expert_specs(ff, half):
    up_spec = pl.BlockSpec((2, 1, ff, half), lambda e, *_: (0, e, 0, 0))
    down_spec = pl.BlockSpec((2, 1, ff // 2, 2 * half), lambda e, *_: (0, e, 0, 0))
    return [up_spec, up_spec, down_spec]


def moe_fwd(off, x, gain, w_r, pos_row, pos_col, exp_col, w_gate, w_up, w_down, rows):
    toks, width = x.shape
    experts, ff = w_gate.shape[1], w_gate.shape[2]
    blk = 128
    tok_out = jax.ShapeDtypeStruct((toks, width), F32)
    small = [x, gain, w_r, pos_row, pos_col, exp_col]
    return pl.pallas_call(
        functools.partial(moe_fwd_kernel, rows=rows, blk=blk),
        out_shape=(tok_out, jax.ShapeDtypeStruct((rows, width), BF16), tok_out, tok_out),
        grid_spec=pltpu.PrefetchScalarGridSpec(
            num_scalar_prefetch=1,
            grid=(experts,),
            in_specs=[whole(a.shape) for a in small] + expert_specs(ff, width // 2),
            out_specs=(whole((toks, width)), whole((rows, width)), whole((toks, width)), whole((toks, width))),
            scratch_shapes=[pltpu.VMEM((rows + blk, width), BF16), pltpu.VMEM((rows + blk, width), F32)],
        ),
        compiler_params=params(48),
        cost_estimate=pl.CostEstimate(flops=30_000_000_000, bytes_accessed=45_000_000, transcendentals=0),
        name="moe_fwd",
    )(off, *small, w_gate, w_up, w_down)


def moe_bwd(off, dx, x, gain, w_r, pos_row, pos_col, exp_row, exp_col, y0, y1, xs, w_gate, w_up, w_down, rows):
    toks, width = x.shape
    experts, ff = w_gate.shape[1], w_gate.shape[2]
    blk = 128
    small = [dx, x, gain, w_r, pos_row, pos_col, exp_row, exp_col, y0, y1, xs]
    out_shapes = (
        jax.ShapeDtypeStruct((toks, width), F32),
        jax.ShapeDtypeStruct((rows, width), F32),
        jax.ShapeDtypeStruct((experts, width), F32),
        jax.ShapeDtypeStruct((1, width), F32),
    )
    return pl.pallas_call(
        functools.partial(moe_bwd_kernel, rows=rows, blk=blk),
        out_shape=out_shapes,
        grid_spec=pltpu.PrefetchScalarGridSpec(
            num_scalar_prefetch=1,
            grid=(experts,),
            in_specs=[whole(a.shape) for a in small] + expert_specs(ff, width // 2),
            out_specs=tuple(whole(s.shape) for s in out_shapes),
            scratch_shapes=[
                pltpu.VMEM((rows + blk, width), BF16),
                pltpu.VMEM((rows + blk, width), BF16),
                pltpu.VMEM((rows + blk, width), F32),
            ],
        ),
        compiler_params=params(60),
        cost_estimate=pl.CostEstimate(flops=50_000_000_000, bytes_accessed=50_000_000, transcendentals=0),
        name="moe_bwd",
    )(off, *small, w_gate, w_up, w_down)


def expert_dw_kernel(off, fs, lr_ref, xs_hbm, dys_hbm, wg_ref, wu_ref, wd_ref, mg_ref, mu_ref, md_ref, *refs, blk, alias):
    refs = refs[3:] if alias else refs
    og_ref, ou_ref, od_ref, xbuf, dbuf, sems, acc_g, acc_u, acc_d = refs
    expert = pl.program_id(0)
    experts = pl.num_programs(0)
    seqs = xs_hbm.shape[0]
    ff, half = acc_g.shape
    mine = fs[0]

    def copies(e, slot, go):
        at = 0
        for s in range(seqs):
            start = pl.multiple_of(off[s, e], TILE)
            count = pl.multiple_of(off[s, e + 1] - off[s, e], TILE)
            dst = pl.multiple_of(at, TILE)

            @pl.when(count > 0)
            def _():
                for hbm, buf, k in ((xs_hbm, xbuf, 0), (dys_hbm, dbuf, 1)):
                    copy = pltpu.make_async_copy(hbm.at[s, pl.ds(start, count), :], buf.at[slot, pl.ds(dst, count), :], sems.at[slot, k])
                    if go:
                        copy.start()
                    else:
                        copy.wait()

            at = at + count
        return at

    slot = lax.rem(expert, 2)

    @pl.when(expert == 0)
    def _():
        copies(0, 0, True)

    @pl.when(expert + 1 < experts)
    def _():
        copies(expert + 1, 1 - slot, True)

    total = pl.multiple_of(copies(expert, slot, False), TILE)
    xbuf[slot, pl.ds(total, blk), :] = jnp.zeros((blk, xbuf.shape[2]), BF16)
    dbuf[slot, pl.ds(total, blk), :] = jnp.zeros((blk, dbuf.shape[2]), F32)
    fill(acc_g, 0)
    fill(acc_u, 0)
    fill(acc_d, 0)
    w_gate = side_by_side(wg_ref)
    w_up = side_by_side(wu_ref)
    w_down = get(wd_ref).reshape(w_gate.shape)

    def body(i, carry):
        at = pl.multiple_of(i * blk, blk)
        xs = xbuf[slot, pl.ds(at, blk), :]
        own = xbuf[slot, pl.ds(at, blk), pl.ds(pl.multiple_of(mine * half, half), half)]
        dys = dbuf[slot, pl.ds(at, blk), :].astype(BF16)
        gate = dot_nt(w_gate, xs)
        up = dot_nt(w_up, xs)
        d_hidden = dot_nt(w_down, dys)
        d_gate, d_up, act = glu_bwd(gate, up, d_hidden)
        hidden = (act * up).astype(BF16)
        put(acc_g, get(acc_g) + dot(d_gate, own))
        put(acc_u, get(acc_u) + dot(d_up, own))
        hidden_own = jnp.where(mine == 0, hidden[: ff // 2], hidden[ff // 2 :])
        put(acc_d, get(acc_d) + dot(hidden_own, dys))
        return carry

    lax.fori_loop(0, (total + blk - 1) // blk, body, 0)
    for out, master, acc in ((og_ref, mg_ref, acc_g), (ou_ref, mu_ref, acc_u), (od_ref, md_ref, acc_d)):
        put(out, get(master) - get(lr_ref) * get(acc).reshape(out.shape))


def expert_dw(layer, off, fs, lr, xs, dys, w_gate, w_up, w_down, m_gate, m_up, m_down, prev):
    seqs, _, width = xs.shape
    _, experts, ff, half = m_gate.shape
    blk = 256
    most = seqs * ((width + TILE - 1) // TILE * TILE)
    any_spec = pl.BlockSpec(memory_space=pl.ANY)
    up_master = pl.BlockSpec((1, 1, ff, half), lambda e, *_: (layer, e, 0, 0))
    down_master = pl.BlockSpec((1, 1, ff // 2, width), lambda e, *_: (layer, e, 0, 0))
    masters = [up_master, up_master, down_master]
    alias = prev is not None
    in_specs = [whole(lr.shape), any_spec, any_spec] + expert_specs(ff, half) + masters
    in_specs += [any_spec] * 3 if alias else []
    return pl.pallas_call(
        functools.partial(expert_dw_kernel, blk=blk, alias=alias),
        out_shape=tuple(jax.ShapeDtypeStruct(m.shape, F32) for m in (m_gate, m_up, m_down)),
        grid_spec=pltpu.PrefetchScalarGridSpec(
            num_scalar_prefetch=2,
            grid=(experts,),
            in_specs=in_specs,
            out_specs=tuple(masters),
            scratch_shapes=[
                pltpu.VMEM((2, most + blk, width), BF16),
                pltpu.VMEM((2, most + blk, width), F32),
                pltpu.SemaphoreType.DMA((2, 2)),
                pltpu.VMEM((ff, half), F32),
                pltpu.VMEM((ff, half), F32),
                pltpu.VMEM((ff // 2, width), F32),
            ],
        ),
        input_output_aliases={11: 0, 12: 1, 13: 2} if alias else {},
        compiler_params=params(62),
        cost_estimate=pl.CostEstimate(flops=90_000_000_000, bytes_accessed=150_000_000, transcendentals=0),
        name="expert_dw",
    )(off, fs, lr, xs, dys, w_gate, w_up, w_down, m_gate, m_up, m_down, *(prev or ()))


def pieces(total, size):
    edges = [*range(0, total, size), total]
    return list(zip(edges, edges[1:]))


def staggered(items, first, second):
    held = None
    for item in items:
        made = first(item)
        if held is not None:
            second(*held)
        held = (item, made)
    second(*held)


def own_first(x, mine):
    lower, upper = pair_of(x, COL)
    return jnp.where(mine == 0, x, jnp.concatenate([upper, lower], axis=COL))


def sublane_groups(x):
    return x.reshape(-1, SUBLANES, x.shape[COL])


def both_cores(refs, lo, hi):
    return jnp.concatenate([ref[lo:hi] for ref in refs], axis=COL)


def head_kernel(fs, x_ref, gain_ref, lab_ref, wa_ref, wb_ref, fin_out, lse_out, dx_out, dg_out, loss_out, fin_s, top_s, sum_s, pick_s, acc_s, *, tokens_all):
    sweep = pl.program_id(0)
    step = pl.program_id(1)
    last = pl.num_programs(1) - 1
    tile = wa_ref.shape[ROW]
    mine = fs[0]
    parts = pieces(tile, HEAD_PIECE)

    @pl.when((sweep == 0) & (step == 0))
    def _():
        fin = rms_norm(get(x_ref), get(gain_ref))
        put(fin_out, fin)
        put(fin_s, own_first(fin, mine).T)
        fill(top_s, NEG)
        fill(sum_s, 0)
        fill(pick_s, 0)
        fill(acc_s, 0)

    def logits_of(part):
        return dot(both_cores((wa_ref, wb_ref), *part), get(fin_s)) * LOG2E

    def take_sums(part, logits):
        grouped = sublane_groups(logits)
        old = get(top_s)
        new = jnp.maximum(old, jnp.max(grouped, axis=ROW))
        put(sum_s, get(sum_s) * jnp.exp2(old - new) + jnp.sum(jnp.exp2(grouped - new), axis=ROW))
        put(top_s, new)

    @pl.when(sweep == 0)
    def _():
        staggered(parts, logits_of, take_sums)

    @pl.when((sweep == 0) & (step == last))
    def _():
        top = jnp.max(get(top_s), axis=ROW, keepdims=True)
        total = axis_sum(get(sum_s) * jnp.exp2(get(top_s) - top), ROW)
        put(lse_out, jnp.broadcast_to(top + jnp.log2(total), lse_out.shape))

    def gradient(part):
        logits = logits_of(part)
        prob = jnp.exp2(logits - (lse_out[:1] + jnp.log2(jnp.float32(tokens_all))))
        hit = iota(logits.shape, ROW) == get(lab_ref) - (step * tile + part[0])
        put(pick_s, get(pick_s) + jnp.sum(sublane_groups(keep(hit, logits)), axis=ROW))
        return (prob - jnp.where(hit, 1.0 / tokens_all, 0.0)).astype(BF16)

    def add_gradient(part, grad):
        put(acc_s, get(acc_s) + dot_tn(grad, both_cores((wa_ref, wb_ref), *part)))

    @pl.when(sweep == 1)
    def _():
        staggered(parts, gradient, add_gradient)

    @pl.when((sweep == 1) & (step == last))
    def _():
        per_tok = (lse_out[:1] - axis_sum(get(pick_s), ROW)) * (LN2 / tokens_all)
        put(loss_out, jnp.broadcast_to(axis_sum(per_tok, COL), loss_out.shape))
        d_fin = own_first(get(acc_s), mine).astype(BF16).astype(F32)
        d_x, d_gain = rms_norm_bwd(get(x_ref), get(gain_ref), d_fin)
        put(dx_out, d_x)
        put(dg_out, d_gain)


def head(fs, x, gain, labels, w_own, w_other, tokens_all):
    toks, width = x.shape
    vocab, half = w_own.shape
    tile = vocab // HEAD_STEPS
    out_shapes = (
        jax.ShapeDtypeStruct((toks, width), BF16),
        jax.ShapeDtypeStruct((LSE_ROWS, toks), F32),
        jax.ShapeDtypeStruct((toks, width), F32),
        jax.ShapeDtypeStruct((1, width), F32),
        jax.ShapeDtypeStruct((1, width), F32),
    )
    small = [x, gain, labels]
    w_spec = pl.BlockSpec((tile, half), lambda p, i, *_: (i, 0))
    return pl.pallas_call(
        functools.partial(head_kernel, tokens_all=tokens_all),
        out_shape=out_shapes,
        grid_spec=pltpu.PrefetchScalarGridSpec(
            num_scalar_prefetch=1,
            grid=(2, HEAD_STEPS),
            in_specs=[whole(a.shape) for a in small] + [w_spec, w_spec],
            out_specs=tuple(whole(s.shape) for s in out_shapes),
            scratch_shapes=[pltpu.VMEM((width, toks), BF16)] + [pltpu.VMEM((SUBLANES, toks), F32)] * 3 + [pltpu.VMEM((toks, width), F32)],
        ),
        compiler_params=params(56),
        cost_estimate=pl.CostEstimate(flops=55_000_000_000, bytes_accessed=70_000_000, transcendentals=0),
        name="head_own",
    )(fs, *small, w_own, w_other)


def head_dw_kernel(fs, fin_ref, lse_ref, lab_ref, wa_ref, wb_ref, own_out, oth_out, fin_s, fin_t, *, tokens_all):
    tile, half = wa_ref.shape
    seqs = fin_s.shape[0]
    mine = fs[0]
    base = (fs[1] * pl.num_programs(0) + pl.program_id(0)) * tile
    parts = pieces(tile, DW_PIECE)
    fill(own_out, 0)
    fill(oth_out, 0)

    @pl.when(pl.program_id(0) == 0)
    def _():
        for s in range(seqs):
            fin = own_first(fin_ref[mine * seqs + s], mine)
            fin_s[s] = fin
            fin_t[s] = fin.T

    def body(s, carry):
        lse = lse_ref[mine * seqs + s, :1] + jnp.log2(jnp.float32(tokens_all))
        lab = lab_ref[mine * seqs + s] - base

        def gradient(part):
            logits = dot(both_cores((wa_ref, wb_ref), *part), fin_t[s]) * LOG2E
            hit = iota(logits.shape, ROW) == lab - part[0]
            return (jnp.exp2(logits - lse) - jnp.where(hit, 1.0 / tokens_all, 0.0)).astype(BF16)

        def add_gradient(part, grad):
            rows = slice(*part)
            own_out[rows] += dot(grad, fin_s[s, :, :half])
            oth_out[rows] += dot(grad, fin_s[s, :, half:])

        staggered(parts, gradient, add_gradient)
        return carry

    lax.fori_loop(0, seqs, body, 0)


def head_dw(fs, fin, lse, labels, w_own, w_other, tokens_all):
    seqs, toks, width = fin.shape
    vocab, half = w_own.shape
    tile = vocab // HEAD_STEPS
    steps = HEAD_STEPS // (seqs // 2)
    out = jax.ShapeDtypeStruct((steps * tile, half), F32)
    out_spec = pl.BlockSpec((tile, half), lambda i, *_: (i, 0))
    w_spec = pl.BlockSpec((tile, half), lambda i, f: (f[1] * steps + i, 0))
    return pl.pallas_call(
        functools.partial(head_dw_kernel, tokens_all=tokens_all),
        out_shape=(out, out),
        grid_spec=pltpu.PrefetchScalarGridSpec(
            num_scalar_prefetch=1,
            grid=(steps,),
            in_specs=[whole(fin.shape), whole(lse.shape), whole(labels.shape), w_spec, w_spec],
            out_specs=(out_spec, out_spec),
            scratch_shapes=[pltpu.VMEM((seqs // 2, toks, width), BF16), pltpu.VMEM((seqs // 2, width, toks), BF16)],
        ),
        compiler_params=params(56),
        cost_estimate=pl.CostEstimate(flops=40_000_000_000, bytes_accessed=40_000_000, transcendentals=0),
        name="head_dw",
    )(fs, fin, lse, labels, w_own, w_other)


def head_upd_kernel(fs, lr_ref, own_ref, recv_ref, m_ref, new_out):
    put(new_out, get(m_ref) - get(lr_ref) * (get(own_ref) + get(recv_ref)))


def head_upd(fs, lr, own, received, master):
    rows, half = own.shape
    tile = master.shape[ROW] // HEAD_STEPS
    steps = rows // tile
    spec = pl.BlockSpec((tile, half), lambda i, *_: (i, 0))
    return pl.pallas_call(
        head_upd_kernel,
        out_shape=jax.ShapeDtypeStruct((rows, half), F32),
        grid_spec=pltpu.PrefetchScalarGridSpec(
            num_scalar_prefetch=1,
            grid=(steps,),
            in_specs=[whole(lr.shape), spec, spec, pl.BlockSpec((tile, half), lambda i, f: (f[1] * steps + i, 0))],
            out_specs=spec,
        ),
        compiler_params=params(48),
        cost_estimate=pl.CostEstimate(flops=8_000_000_000, bytes_accessed=33_000_000, transcendentals=0),
        name="head_upd",
    )(fs, lr, own, received, master)


def embed_upd_kernel(bounds, keys, perm, lr_ref, rows_ref, m_ref, new_out, wide_s):
    step = pl.program_id(0)
    rows = m_ref.shape[0]

    @pl.when(step == 0)
    def _():
        put(wide_s, get(rows_ref).astype(F32) * get(lr_ref))

    put(new_out, get(m_ref))

    def body(j, carry):
        at = new_out.at[pl.ds(keys[j] - step * rows, 1)]
        put(at, get(at) - get(wide_s.at[pl.ds(perm[j], 1)]))
        return carry

    lax.fori_loop(bounds[step], bounds[step + 1], body, 0)


def embed_upd(bounds, keys, perm, lr, grads, master, rows):
    vocab, width = master.shape
    return pl.pallas_call(
        embed_upd_kernel,
        out_shape=jax.ShapeDtypeStruct((vocab, width), F32),
        grid_spec=pltpu.PrefetchScalarGridSpec(
            num_scalar_prefetch=3,
            grid=(vocab // rows,),
            in_specs=[
                whole(lr.shape),
                whole(grads.shape),
                pl.BlockSpec((rows, width), lambda i, *_: (i, 0)),
            ],
            out_specs=pl.BlockSpec((rows, width), lambda i, *_: (i, 0)),
            scratch_shapes=[pltpu.VMEM(grads.shape, F32)],
        ),
        compiler_params=params(48),
        cost_estimate=pl.CostEstimate(flops=25_000_000_000, bytes_accessed=66_000_000, transcendentals=0),
        name="embed_upd",
    )(bounds, keys, perm, lr, grads, master)


def rope_tables(positions):
    inv_freq = ROPE_THETA ** (-jnp.arange(0, HEAD_DIM, 2, dtype=F32) / HEAD_DIM)
    angle = positions.astype(F32)[:, None] * inv_freq
    cos, sin = jnp.cos(angle), jnp.sin(angle)
    return jnp.concatenate([cos, cos], axis=COL), jnp.concatenate([-sin, sin], axis=COL)


def half_turn(x):
    return pltpu.roll(x, HEAD_DIM // 2, COL)


def rope(x, cos, sin):
    return x * cos + half_turn(x) * sin


def rope_bwd(dx, cos, sin):
    return dx * cos + half_turn(dx * sin)


def qkv_heads(x, gain, weights, cos, sin, q_width):
    normed = rms_norm(x, gain)
    all_heads = jnp.split(dot(normed, weights), weights.shape[COL] // HEAD_DIM, axis=COL)
    count = q_width // HEAD_DIM
    queries = [rope(q, cos, sin).astype(BF16) for q in all_heads[:count]]
    key, value = all_heads[count:]
    return normed, queries, rope(key, cos, sin).astype(BF16), value.astype(BF16)


def attn_probs(query, key):
    scores = dot_nt(query, key) * HEAD_DIM ** -0.5
    scores = jnp.where(iota(scores.shape, ROW) >= iota(scores.shape, COL), scores, NEG)
    raised = jnp.exp(scores - jnp.max(scores, axis=COL, keepdims=True))
    return raised / axis_sum(raised, COL)


def attn_fwd_kernel(x_ref, gain_ref, cos_ref, sin_ref, w_ref, out_ref, *, q_width, in_width):
    x = get(x_ref)
    weights = get(w_ref).reshape(x.shape[COL], -1)
    _, queries, key, value = qkv_heads(x, get(gain_ref), weights[:, :in_width], get(cos_ref), get(sin_ref), q_width)
    mixed = [dot(attn_probs(query, key).astype(BF16), value).astype(BF16) for query in queries]
    put(out_ref, x + dot(jnp.concatenate(mixed, axis=COL), weights[:, in_width:]))


def attn_bwd_kernel(dx_ref, x_ref, gain_ref, cos_ref, sin_ref, dwr_ref, dgm_ref, dgf_ref, loss_ref, w_ref, dx_out, dw_out, *, q_width, in_width):
    x = get(x_ref)
    d_out = get(dx_ref)
    gain, cos, sin = get(gain_ref), get(cos_ref), get(sin_ref)
    weights = get(w_ref).reshape(x.shape[COL], -1)
    half = x.shape[COL] // 2
    normed, queries, key, value = qkv_heads(x, gain, weights[:, :in_width], cos, sin, q_width)
    d_proj = d_out.astype(BF16)
    d_mixed = jnp.split(dot_nt(d_proj, weights[:, in_width:]).astype(BF16), len(queries), axis=COL)
    mixed, d_heads = [], []
    d_key = d_value = None
    for query, d_mix in zip(queries, d_mixed):
        probs = attn_probs(query, key)
        rounded = probs.astype(BF16)
        mixed.append(dot(rounded, value).astype(BF16))
        d_probs = dot_nt(d_mix, value)
        d_scores = (probs * (d_probs - axis_sum(d_probs * probs, COL)) * HEAD_DIM ** -0.5).astype(BF16)
        d_heads.append(rope_bwd(dot(d_scores, key), cos, sin).astype(BF16))
        more_key, more_value = dot_tn(d_scores, query), dot_tn(rounded, d_mix)
        d_key = more_key if d_key is None else d_key + more_key
        d_value = more_value if d_value is None else d_value + more_value
    d_heads += [rope_bwd(d_key, cos, sin).astype(BF16), d_value.astype(BF16)]
    d_in = jnp.concatenate(d_heads, axis=COL)
    d_weights = jnp.concatenate([dot_tn(normed, d_in), dot_tn(jnp.concatenate(mixed, axis=COL), d_proj)], axis=COL)
    d_x, d_gain = rms_norm_bwd(x, gain, dot_nt(d_in, weights[:, :in_width]).astype(BF16).astype(F32))
    put(dx_out, d_out + d_x)
    for core, d_half in enumerate(pair_of(d_weights, ROW)):
        dw_out[core, :half] = d_half
    small = jnp.concatenate([get(dwr_ref), d_gain, get(dgm_ref), get(dgf_ref), get(loss_ref)], axis=ROW)
    per_row = d_weights.shape[COL] // half
    for i in range(small.shape[ROW]):
        row, at = half + i // per_row, i % per_row * half
        for core, part in enumerate(pair_of(small[i : i + 1], COL)):
            dw_out[core, row : row + 1, at : at + half] = part


def attn_specs(arrays, w_all, layer):
    spec = pl.BlockSpec((2, 1, *w_all.shape[2:]), lambda i: (0, layer, 0, 0))
    return [whole(a.shape) for a in arrays] + [spec]


def attn_fwd(layer, x, gain, cos, sin, w_all, q_width, in_width):
    small = [x, gain, cos, sin]
    return pl.pallas_call(
        functools.partial(attn_fwd_kernel, q_width=q_width, in_width=in_width),
        out_shape=jax.ShapeDtypeStruct(x.shape, F32),
        grid=(1,),
        in_specs=attn_specs(small, w_all, layer),
        out_specs=whole(x.shape),
        compiler_params=params(48),
        cost_estimate=pl.CostEstimate(flops=8_000_000_000, bytes_accessed=5_000_000, transcendentals=0),
        name="attn_fwd",
    )(*small, w_all)


def attn_bwd(layer, dx, x, gain, cos, sin, d_router, d_mlp, d_final, loss, w_all, q_width, in_width):
    small = [dx, x, gain, cos, sin, d_router, d_mlp, d_final, loss]
    half, wide = w_all.shape[2:]
    tail = -(-(d_router.shape[ROW] + 4) // (wide // half) // SUBLANES) * SUBLANES
    grads = jax.ShapeDtypeStruct((2, half + tail, wide), F32)
    return pl.pallas_call(
        functools.partial(attn_bwd_kernel, q_width=q_width, in_width=in_width),
        out_shape=(jax.ShapeDtypeStruct(x.shape, F32), grads),
        grid=(1,),
        in_specs=attn_specs(small, w_all, layer),
        out_specs=(whole(x.shape), whole(grads.shape)),
        compiler_params=params(60),
        cost_estimate=pl.CostEstimate(flops=15_000_000_000, bytes_accessed=10_000_000, transcendentals=0),
        name="attn_bwd",
    )(*small, w_all)


def routing(experts_of, experts):
    toks = experts_of.shape[0]
    hot = (experts_of[:, :, None] == jnp.arange(experts, dtype=I32)).astype(F32)
    both = hot[:, 0] + hot[:, 1]
    before = iota((toks, toks), 0) > iota((toks, toks), 1)
    ahead = dot(before.astype(BF16), both.astype(BF16))
    counts = jnp.sum(both, axis=0).astype(I32)
    padded = (counts + TILE - 1) // TILE * TILE
    upto = iota((experts + 1, experts), 0) > iota((experts + 1, experts), 1)
    starts = jnp.sum(jnp.where(upto, padded[None, :], 0), axis=1)
    place = starts[:experts].astype(F32) + ahead
    return jnp.sum(hot * place[:, None, :], axis=2).astype(I32), starts


def solution(mesh):
    device_count = mesh.shape['rep'] * mesh.shape['fsdp']
    both = ('rep', 'fsdp')
    batch_spec = P(both)
    layer_spec = P(None, 'fsdp')
    expert_spec = P(None, None, 'fsdp')
    param_specs = (P('fsdp'), layer_spec, layer_spec, layer_spec, layer_spec, layer_spec, layer_spec, layer_spec, expert_spec, expert_spec, expert_spec, P('fsdp'), P('fsdp'))
    in_specs = (batch_spec, batch_spec, batch_spec, P(None, both), P()) + param_specs
    out_specs = param_specs + (P(),)

    def step(tok_ids, tok_labels, tok_pos, expert_idx, learn_rate, embedding, w_query, w_key, w_value, w_attn_out, g_attn, g_mlp, w_router, w_gate, w_up, w_down, g_final, w_head):
        layers, half, q_width = w_query.shape
        kv_width = w_key.shape[2]
        width = 2 * half
        toks = tok_ids.shape[1]
        experts = w_router.shape[2]
        tokens_all = toks * device_count
        vocab_share = embedding.shape[0]
        rows = 2 * toks + experts * TILE
        me = lax.axis_index('fsdp')
        pair = lax.axis_index('rep')
        fs = jnp.stack([me, pair]).astype(I32)
        lr = learn_rate.reshape(1, 1)
        swap = [(0, 1), (1, 0)]

        m_gate = jnp.swapaxes(w_gate, 2, 3)
        m_up = jnp.swapaxes(w_up, 2, 3)
        m_head = w_head.T

        experts_of = expert_idx[:, 0]
        placed = [routing(experts_of[l], experts) for l in range(layers)]
        starts = jnp.stack([s for _, s in placed])
        ints = jnp.concatenate([tok_ids[0], tok_labels[0], starts.reshape(-1)]).astype(F32)
        misc = jnp.concatenate([jnp.swapaxes(w_router, 1, 2).reshape(layers * experts, half), g_attn, g_mlp, g_final[None]])
        misc = misc.astype(BF16).astype(F32).reshape(-1)
        packed = jnp.concatenate([misc, ints])
        n_misc = misc.shape[0]
        packed = jnp.pad(packed, (0, -packed.shape[0] % 1024)).reshape(-1, 128)
        known = lax.all_gather(packed, both).reshape(device_count, -1)
        two = lax.dynamic_slice_in_dim(known, pair * 2, 2, 0)[:, :n_misc].reshape(2, -1, half)
        misc_all = jnp.concatenate([two[0], two[1]], axis=1)
        w_r = [misc_all[l * experts : (l + 1) * experts].astype(BF16) for l in range(layers)]
        base = layers * experts
        gain_attn = [misc_all[base + l][None] for l in range(layers)]
        gain_mlp = [misc_all[base + layers + l][None] for l in range(layers)]
        gain_final = misc_all[base + 2 * layers][None]
        known_ints = known[:, n_misc : n_misc + ints.shape[0]].astype(I32)
        ids_all = known_ints[:, :toks]
        labels_all = known_ints[:, toks : 2 * toks]
        starts_all = known_ints[:, 2 * toks :].reshape(device_count, layers, experts + 1)

        attn_pack = jnp.concatenate([w_query, w_key, w_value, w_attn_out], axis=2).astype(BF16)
        attn_all = lax.all_gather(attn_pack, 'fsdp')

        def gather(x):
            return lax.all_gather(x.astype(BF16), 'fsdp')

        expert_w = [(gather(m_gate[l]), gather(m_up[l]), gather(w_down[l])) for l in range(layers)]
        head_w = (m_head.astype(BF16),)
        head_w += (lax.ppermute(head_w[0], 'fsdp', swap),)

        partner_ids = lax.dynamic_index_in_dim(ids_all, pair * 2 + 1 - me, 0, keepdims=False)
        wanted = jnp.concatenate([tok_ids[0], partner_ids]) - me * vocab_share
        taken = jnp.take(embedding, jnp.clip(wanted, 0, vocab_share - 1), axis=0).astype(BF16)
        sent = lax.ppermute(taken[toks:], 'fsdp', swap)
        is_mine = (wanted[:toks] >= 0) & (wanted[:toks] < vocab_share)
        x = jnp.where(is_mine[:, None], taken[:toks], sent).astype(F32)

        tables = rope_tables(tok_pos[0])
        widths = (q_width, q_width + 2 * kv_width)

        xs_all, kept = [], []
        for l in range(layers):
            mid = attn_fwd(l, x, gain_attn[l], *tables, attn_all, *widths)
            pos, start = placed[l]
            out, xs, y0, y1 = moe_fwd(start, mid, gain_mlp[l], w_r[l], pos.T, pos, experts_of[l], *expert_w[l], rows)
            kept.append((x, mid, xs, y0, y1))
            xs_all.append(lax.all_gather(xs, both))
            x = out

        fin, lse, dx, d_final, loss = head(fs, x, gain_final, tok_labels, *head_w, tokens_all)
        fin_all = lax.all_gather(fin, both)
        lse_all = lax.all_gather(lse, both)

        dys_all = [None] * layers
        reduced = [None] * layers
        new_head = None
        for l in reversed(range(layers)):
            x, mid, xs, y0, y1 = kept[l]
            pos, start = placed[l]
            dx, dys, d_router, d_mlp = moe_bwd(start, dx, mid, gain_mlp[l], w_r[l], pos.T, pos, experts_of[l].T, experts_of[l], y0, y1, xs, *expert_w[l], rows)
            dys_all[l] = lax.all_gather(dys, both)
            if new_head is None:
                fin_all, _ = lax.optimization_barrier((fin_all, dx))
                own_grad, other_grad = head_dw(fs, fin_all, lse_all, labels_all[:, None], *head_w, tokens_all)
                dx, _ = lax.optimization_barrier((dx, own_grad))
            dx, grads = attn_bwd(l, dx, x, gain_attn[l], *tables, d_router, d_mlp, d_final, loss, attn_all, *widths)
            if new_head is None:
                quarter = head_upd(fs, lr, own_grad, lax.ppermute(other_grad, 'fsdp', swap), m_head)
                new_head = lax.all_gather(quarter, 'rep', tiled=True)
            reduced[l] = lax.psum(lax.psum_scatter(grads, 'fsdp', scatter_dimension=0, tiled=False), 'rep')

        d_rows = lax.all_gather(dx.astype(BF16), both).reshape(tokens_all, width)

        new_experts = None
        for l in reversed(range(layers)):
            new_experts = expert_dw(l, starts_all[:, l], fs, lr, xs_all[l], dys_all[l], *expert_w[l], m_gate, m_up, w_down, new_experts)

        block = 1336
        local_id = ids_all.reshape(-1) - me * vocab_share
        key = jnp.where((local_id >= 0) & (local_id < vocab_share), local_id, vocab_share)
        keys, perm = lax.sort((key, lax.iota(I32, tokens_all)), num_keys=1)
        edges = jnp.arange(vocab_share // block + 1, dtype=I32) * block
        bounds = jnp.sum(key[None, :] < edges[:, None], axis=1).astype(I32)
        new_embedding = embed_upd(bounds, keys, perm, lr, d_rows, embedding, block)

        def update(master, pick):
            return master - learn_rate * jnp.stack([pick(reduced[l]) for l in range(layers)])

        def tail_of(r, first, count):
            return r[half:].reshape(-1)[first * half : (first + count) * half].reshape(count, half)

        v_at = q_width + kv_width
        new_query = update(w_query, lambda r: r[:half, :q_width])
        new_key = update(w_key, lambda r: r[:half, q_width:v_at])
        new_value = update(w_value, lambda r: r[:half, v_at : v_at + kv_width])
        new_attn_out = update(w_attn_out, lambda r: r[:half, v_at + kv_width :])
        new_router = update(w_router, lambda r: tail_of(r, 0, experts).T)
        new_g_attn = update(g_attn, lambda r: tail_of(r, experts, 1)[0])
        new_g_mlp = update(g_mlp, lambda r: tail_of(r, experts + 1, 1)[0])
        new_final = g_final - learn_rate * tail_of(reduced[0], experts + 2, 1)[0]
        both_loss = tail_of(reduced[0], experts + 3, 1)[0, 0]
        new_gate, new_up, new_down = new_experts
        return (new_embedding, new_query, new_key, new_value, new_attn_out, new_g_attn, new_g_mlp, new_router,
                jnp.swapaxes(new_gate, 2, 3), jnp.swapaxes(new_up, 2, 3), new_down, new_final, new_head.T, both_loss)

    return jax.shard_map(step, mesh=mesh, in_specs=in_specs, out_specs=out_specs, check_vma=False)
```

profile of v0, /device:TPU:0, one launch (start us, length us, event | category | flops | bytes accessed | tf_op | source)
XLA Modules:
  0.0 1259.8 jit_solution(6402794752040434194)
XLA Ops:
  13.0 10.1 bitcast_convert_fusion.2
  23.1 5.1 fusion.24
  28.3 11.1 bitcast_convert_fusion.1
  39.3 7.3 fusion.23
  46.7 10.2 convert.59
  57.0 6.3 fusion.22
  64.5 20.6 %bitcast_convert_fusion.wa_ref = bf16[32064,256]{1,0:T(8,128)(2,1)} fusion(f32[256,32064]{0,1:T(8,128)} %param.35), kind=kLoop, calls=%fused_computation.99 | loop fusion | flops 8208384 | bytes 49250304 | tf_op jit(solution)/shard_map/convert_element_type | solution.py:849
  87.4 41.1 %all_gather.76 = f32[8,88,128]{2,1,0:T(8,128)S(1)} all-gather(f32[1,88,128]{2,1,0:T(8,128)S(1)} %fusion.8), channel_id=1, replica_groups=mesh['rep'=4,'fsdp'=2] {'rep','fsdp'}, dimensions={0}, use_global_device_ids=true | all-gather | bytes 405504 | tf_op jit(solution)/shard_map/all_gather | solution.py:829
  129.3 16.9 %gather_fusion = bf16[1024,512]{1,0:T(8,128)(2,1)S(1)} fusion(f32[16032,512]{1,0:T(8,128)} %m_ref.1, s32[1024]{0:T(1024)S(1)} %broadcast_clamp_fusion), kind=kCustom, calls=%fused_computation | custom fusion | bytes 2101248 | tf_op jit(solution)/shard_map/jit(_take)/gather | solution.py:854
  162.0 43.6 %moe_fwd.2 = (f32[512,512]{1,0:T(8,128)S(1)}, bf16[1280,512]{1,0:T(8,128)(2,1)}, f32[512,512]{1,0:T(8,128)S(1)}, f32[512,512]{1,0:T(8,128)S(1)}) custom-call(s32[17]{0:T(128)S(1)} %select_reduce_fusion.3.off, f32[512,512]{1,0:T(8,128)S(1)} %copy-done.22, f32[1,512]{1,0:T(1,128)S(1)} %get-tuple-element.115.gain_ref, ...), custom_call_target="tpu_custom_call" | custom-call | flops 30000001024 | bytes 45000000 | tf_op jit(solution)/shard_map/moe_fwd/pallas_call | solution.py:267
  212.8 30.5 %moe_fwd.3 = (f32[512,512]{1,0:T(8,128)S(1)}, bf16[1280,512]{1,0:T(8,128)(2,1)}, f32[512,512]{1,0:T(8,128)S(1)}, f32[512,512]{1,0:T(8,128)S(1)}) custom-call(s32[17]{0:T(128)S(1)} %select_reduce_fusion.2.off, f32[512,512]{1,0:T(8,128)S(1)} %attn_fwd.3.x_ref, f32[1,512]{1,0:T(1,128)S(1)} %get-tuple-element.113.gain_ref, ...), custom_call_target="tpu_custom_call" | custom-call | flops 30000001024 | bytes 45000000 | tf_op jit(solution)/shard_map/moe_fwd/pallas_call | solution.py:267
  246.2 78.6 %head_own.1 = (bf16[512,512]{1,0:T(8,128)(2,1)}, f32[72,512]{1,0:T(8,128)}, f32[512,512]{1,0:T(8,128)}, f32[1,512]{1,0:T(1,128)}, f32[1,512]{1,0:T(1,128)}) custom-call(s32[2]{0:T(128)} %pad_add_fusion.1.fs, f32[512,512]{1,0:T(8,128)} %copy-done.29, f32[1,512]{1,0:T(1,128)} %get-tuple-element.112.gain_ref, s32[1,512]{1,0:T(1,128)} %lab_ref.1, ...), custom_call_target="tpu_custom_call" | custom-call | flops 54999998464 | bytes 70000000 | tf_op jit(solution)/shard_map/head_own/pallas_call | solution.py:522
  326.9 45.1 %moe_bwd.2 = (f32[512,512]{1,0:T(8,128)}, f32[1280,512]{1,0:T(8,128)}, f32[16,512]{1,0:T(8,128)}, f32[1,512]{1,0:T(1,128)}) custom-call(s32[17]{0:T(128)} %copy-done.16, f32[512,512]{1,0:T(8,128)} %get-tuple-element.55.dx_ref, f32[512,512]{1,0:T(8,128)} %copy-done.24, f32[1,512]{1,0:T(1,128)} %copy-done.14, bf16[16,512]{1,0:T(8,128)(2,1)} %copy-done.8, ...), custom_call_target="tpu_custom_call" | custom-call | flops 49999998976 | bytes 50000000 | tf_op jit(solution)/shard_map/moe_bwd/pallas_call | solution.py:294
  372.0 4.9 all-gather.41.cloned.1.call-done
  376.9 46.1 %head_dw.1 = (f32[8016,256]{1,0:T(8,128)}, f32[8016,256]{1,0:T(8,128)}) custom-call(s32[2]{0:T(128)} %pad_add_fusion.1.fs, bf16[8,512,512]{2,1,0:T(8,128)(2,1)} %bitcast.147, f32[8,72,512]{2,1,0:T(8,128)} %bitcast.148, s32[8,1,512]{2,1,0:T(1,128)} %broadcast_in_dim.65.lab_ref, bf16[32064,256]{1,0:T(8,128)(2,1)} %bitcast_convert_fusion.wa_ref, ...), custom_call_target="tpu_custom_call" | custom-call | flops 40000000000 | bytes 40000000 | tf_op jit(solution)/shard_map/head_dw/pallas_call | solution.py:582
  423.0 10.7 attn_bwd.2
  433.7 44.7 %moe_bwd.3 = (f32[512,512]{1,0:T(8,128)}, f32[1280,512]{1,0:T(8,128)}, f32[16,512]{1,0:T(8,128)}, f32[1,512]{1,0:T(1,128)}) custom-call(s32[17]{0:T(128)} %copy-done.15, f32[512,512]{1,0:T(8,128)} %get-tuple-element.69.dx_ref, f32[512,512]{1,0:T(8,128)} %copy-done.21, f32[1,512]{1,0:T(1,128)} %copy-done.12, bf16[16,512]{1,0:T(8,128)(2,1)} %copy-done.7, ...), custom_call_target="tpu_custom_call" | custom-call | flops 49999998976 | bytes 50000000 | tf_op jit(solution)/shard_map/moe_bwd/pallas_call | solution.py:294
  478.3 10.7 attn_bwd.3
  492.0 4.9 reduce-scatter.3.cloned.1.call-done
  496.9 11.9 reduce-scatter.5.cloned.1.call-done
  512.3 12.2 collective-permute-done.2.recv_ref
  524.5 14.0 %head_upd.1 = f32[8016,256]{1,0:T(8,128)} custom-call(s32[2]{0:T(128)S(1)} %copy-done.17, f32[1,1]{1,0:T(1,128)} %bitcast.105.lr_ref, f32[8016,256]{1,0:T(8,128)} %get-tuple-element.63.own_ref, f32[8016,256]{1,0:T(8,128)} %collective-permute-done.2.recv_ref, f32[32064,256]{1,0:T(8,128)} %bitcast.116), custom_call_target="tpu_custom_call" | custom-call | flops 8000000000 | bytes 33000000 | tf_op jit(solution)/shard_map/head_upd/pallas_call | solution.py:607
  539.3 5.2 sort.15
  547.5 38.4 %embed_upd.1 = f32[16032,512]{1,0:T(8,128)} custom-call(s32[13]{0:T(128)S(1)} %convert_reduce_fusion.bounds, s32[4096]{0:T(1024)S(1)} %get-tuple-element.51.keys, s32[4096]{0:T(1024)S(1)} %get-tuple-element.52.perm, f32[1,1]{1,0:T(1,128)} %bitcast.102.lr_ref, bf16[4096,512]{1,0:T(8,128)(2,1)S(1)} %copy-done.18, f32[16032,512]{1,0:T(8,128)} %m_ref.1), custom_call_target="tpu_custom_call" | custom-call | flops 24999999488 | bytes 66000000 | tf_op jit(solution)/shard_map/embed_upd/pallas_call | solution.py:642
  585.9 30.7 %all-reduce.4.cloned.1.call-done = (f32[264,1280]{1,0:T(8,128)}, f32[264,1280]{1,0:T(8,128)}) async-done(((f32[264,1280]{1,0:T(8,128)}, f32[264,1280]{1,0:T(8,128)}), (f32[264,1280]{1,0:T(8,128)}, f32[264,1280]{1,0:T(8,128)})) %all-reduce.4.cloned.1.call-update) | async-done | bytes 2703376 | tf_op jit(solution)/shard_map/psum | solution.py:891
  628.2 47.9 %all-gather.49.cloned.1.call-done = bf16[10240,512]{1,0:T(8,128)(2,1)} async-done(((bf16[1280,512]{1,0:T(8,128)(2,1)}), bf16[10240,512]{1,0:T(8,128)(2,1)}) %all-gather.49.cloned.1.call-update) | async-done | bytes 10485776 | tf_op jit(solution)/shard_map/all_gather | solution.py:868
  676.0 103.6 %all-gather.51.cloned.1.call-done = f32[10240,512]{1,0:T(8,128)} async-done(((f32[1280,512]{1,0:T(8,128)}), f32[10240,512]{1,0:T(8,128)}) %all-gather.51.cloned.1.call-update) | async-done | bytes 20971536 | tf_op jit(solution)/shard_map/all_gather | solution.py:882
  779.6 89.1 %expert_dw.2 = (f32[2,16,800,256]{3,2,1,0:T(8,128)}, f32[2,16,800,256]{3,2,1,0:T(8,128)}, f32[2,16,400,512]{3,2,1,0:T(8,128)}) custom-call(s32[8,17]{1,0:T(8,128)} %bitcast.140, s32[2]{0:T(128)} %pad_add_fusion.1.fs, f32[1,1]{1,0:T(1,128)} %bitcast.103.lr_ref, bf16[8,1280,512]{2,1,0:T(8,128)(2,1)} %bitcast.146, f32[8,1280,512]{2,1,0:T(8,128)} %bitcast.144, ...), custom_call_target="tpu_custom_call" | custom-call | flops 89999998976 | bytes 150000000 | tf_op jit(solution)/shard_map/expert_dw/pallas_call | solution.py:395
  868.8 73.8 %all-gather.47.cloned.1.call-done = f32[10240,512]{1,0:T(8,128)} async-done(((f32[1280,512]{1,0:T(8,128)}), f32[10240,512]{1,0:T(8,128)}) %all-gather.47.cloned.1.call-update) | async-done | bytes 20971536 | tf_op jit(solution)/shard_map/all_gather | solution.py:882
  942.5 88.5 %expert_dw.3 = (f32[2,16,800,256]{3,2,1,0:T(8,128)}, f32[2,16,800,256]{3,2,1,0:T(8,128)}, f32[2,16,400,512]{3,2,1,0:T(8,128)}) custom-call(s32[8,17]{1,0:T(8,128)} %bitcast.139, s32[2]{0:T(128)} %pad_add_fusion.1.fs, f32[1,1]{1,0:T(1,128)} %bitcast.104.lr_ref, ...), custom_call_target="tpu_custom_call", output_to_operand_aliasing={{0}: (11, {}), {1}: (12, {}), {2}: (13, {})} | custom-call | flops 89999998976 | bytes 150000000 | tf_op jit(solution)/shard_map/expert_dw/pallas_call | solution.py:395
  1031.0 199.3 %all-gather.37.cloned.1.call-done = f32[32064,256]{1,0:T(8,128)} async-done(((f32[8016,256]{1,0:T(8,128)}), f32[32064,256]{1,0:T(8,128)}) %all-gather.37.cloned.1.call-update) | async-done | bytes 32833552 | tf_op jit(solution)/shard_map/all_gather | solution.py:890
  1230.3 22.4 %copy.101 = f32[256,32064]{0,1:T(8,128)} copy(f32[256,32064]{0,1:T(8,128)} %bitcast.117) | data formatting | bytes 65667072
  (249 shorter events, 58.4 us)
Async XLA Ops:
  7.2 146.0 %all-gather.23.cloned.1.call-start = ((), (), s32[]{:S(2)}) async-start(), calls=%async_computation.2 | async-start | bytes 3932160 | tf_op jit(solution)/shard_map/all_gather | solution.py:843
  13.0 147.8 %all-gather.25.cloned.1.call-start = ((), (), s32[]{:S(2)}) async-start(), calls=%async_computation.3 | async-start | bytes 19660800 | tf_op jit(solution)/shard_map/all_gather | solution.py:846
  28.2 132.5 %all-gather.27.cloned.1.call-start = ((), (), s32[]{:S(2)}) async-start(), calls=%async_computation.4 | async-start | bytes 19660800 | tf_op jit(solution)/shard_map/all_gather | solution.py:846
  46.7 114.0 %all-gather.29.cloned.1.call-start = ((), (), s32[]{:S(2)}) async-start(), calls=%async_computation.5 | async-start | bytes 19660800 | tf_op jit(solution)/shard_map/all_gather | solution.py:846
  63.3 149.4 %all-gather.31.cloned.1.call-start = ((), (), s32[]{:S(2)}) async-start(), calls=%async_computation.6 | async-start | bytes 19660800 | tf_op jit(solution)/shard_map/all_gather | solution.py:846
  63.9 148.8 %all-gather.33.cloned.1.call-start = ((), (), s32[]{:S(2)}) async-start(), calls=%async_computation.7 | async-start | bytes 19660800 | tf_op jit(solution)/shard_map/all_gather | solution.py:846
  64.5 148.2 %all-gather.35.cloned.1.call-start = ((), (), s32[]{:S(2)}) async-start(), calls=%async_computation.8 | async-start | bytes 19660800 | tf_op jit(solution)/shard_map/all_gather | solution.py:846
  85.2 161.0 %collective-permute-start.1 = (bf16[32064,256]{1,0:T(8,128)(2,1)}, bf16[32064,256]{1,0:T(8,128)(2,1)}, u32[]{:S(2)}, u32[]{:S(2)}) collective-permute-start(bf16[32064,256]{1,0:T(8,128)(2,1)} %bitcast_convert_fusion.wa_ref), channel_id=1, source_target_pairs={{0,1},{1,0},{2,3},{3,2},{4,5},{5,4},{6,7},{7,6}} | collective-permute-start | bytes 49250312 | tf_op jit(solution)/shard_map/ppermute | solution.py:850
  86.0 286.0 %all-gather.39.cloned.1.call-start = ((), (), s32[]{:S(2)}) async-start(), calls=%async_computation.12 | async-start | bytes 4718592 | tf_op jit(solution)/shard_map/all_gather | solution.py:872
  86.4 238.4 %copy-start = (s32[1,1,512,2]{3,2,1,0:T(8,128)}, s32[1,1,512,2]{3,2,1,0:T(8,128)S(1)}, u32[]{:S(2)}) copy-start(s32[1,1,512,2]{3,2,1,0:T(8,128)S(1)} %copy.85) | copy-start | bytes 12292
  86.7 238.8 %copy-start.1 = (s32[1,1,512,2]{3,2,1,0:T(8,128)}, s32[1,1,512,2]{3,2,1,0:T(8,128)S(1)}, u32[]{:S(2)}) copy-start(s32[1,1,512,2]{3,2,1,0:T(8,128)S(1)} %copy.86) | copy-start | bytes 12292
  87.1 73.7 %copy-start.15 = (s32[17]{0:T(128)}, s32[17]{0:T(128)S(1)}, u32[]{:S(2)}) copy-start(s32[17]{0:T(128)S(1)} %select_reduce_fusion.3.off) | copy-start | bytes 208
  87.3 125.4 %copy-start.16 = (s32[17]{0:T(128)}, s32[17]{0:T(128)S(1)}, u32[]{:S(2)}) copy-start(s32[17]{0:T(128)S(1)} %select_reduce_fusion.2.off) | copy-start | bytes 208
  147.6 4.2 collective-permute-start
  148.6 64.1 %copy-start.5 = (s32[512,2]{1,0:T(8,128)}, s32[512,2]{1,0:T(8,128)S(1)}, u32[]{:S(2)}) copy-start(s32[512,2]{1,0:T(8,128)S(1)} %get-tuple-element.108.pcol_ref) | copy-start | bytes 12292
  324.8 52.1 %all-gather.41.cloned.1.call-start = ((), (), s32[]{:S(2)}) async-start(), calls=%async_computation.13 | async-start | bytes 1327104 | tf_op jit(solution)/shard_map/all_gather | solution.py:873
  326.9 170.0 %reduce-scatter.3.cloned.1.call-start = ((), (), s32[]{:S(2)}) async-start(), calls=%async_computation.9 | async-start | bytes 4055040 | tf_op jit(solution)/shard_map/reduce_scatter | solution.py:891
  489.0 19.8 %reduce-scatter.5.cloned.1.call-start = ((), (), s32[]{:S(2)}) async-start(), calls=%async_computation.10 | async-start | bytes 4055040 | tf_op jit(solution)/shard_map/reduce_scatter | solution.py:891
  489.8 55.5 %all-gather.43.cloned.1.call-start = ((), (), s32[]{:S(2)}) async-start(), calls=%async_computation.14 | async-start | bytes 4718592 | tf_op jit(solution)/shard_map/all_gather | solution.py:893
  491.9 124.7 %all-reduce.4.cloned.1.call-start = ((), (), s32[]{:S(2)}) async-start(), calls=%async_computation.19 | async-start | bytes 5406720 | tf_op jit(solution)/shard_map/psum | solution.py:891
  508.8 167.2 %all-gather.49.cloned.1.call-start = ((), (), s32[]{:S(2)}) async-start(), calls=%async_computation.17 | async-start | bytes 11796480 | tf_op jit(solution)/shard_map/all_gather | solution.py:868
  509.4 270.2 %all-gather.51.cloned.1.call-start = ((), (), s32[]{:S(2)}) async-start(), calls=%async_computation.18 | async-start | bytes 23592960 | tf_op jit(solution)/shard_map/all_gather | solution.py:882
  510.0 358.7 %all-gather.45.cloned.1.call-start = ((), (), s32[]{:S(2)}) async-start(), calls=%async_computation.15 | async-start | bytes 11796480 | tf_op jit(solution)/shard_map/all_gather | solution.py:868
  510.6 432.0 %all-gather.47.cloned.1.call-start = ((), (), s32[]{:S(2)}) async-start(), calls=%async_computation.16 | async-start | bytes 23592960 | tf_op jit(solution)/shard_map/all_gather | solution.py:882
  511.2 719.2 %all-gather.37.cloned.1.call-start = ((), (), s32[]{:S(2)}) async-start(), calls=%async_computation.11 | async-start | bytes 41041920 | tf_op jit(solution)/shard_map/all_gather | solution.py:890
  511.2 13.3 %collective-permute-start.2 = (f32[8016,256]{1,0:T(8,128)}, f32[8016,256]{1,0:T(8,128)}, u32[]{:S(2)}, u32[]{:S(2)}) collective-permute-start(f32[8016,256]{1,0:T(8,128)} %get-tuple-element.87), channel_id=1, source_target_pairs={{0,1},{1,0},{2,3},{3,2},{4,5},{5,4},{6,7},{7,6}} | collective-permute-start | bytes 24625160 | tf_op jit(solution)/shard_map/ppermute | solution.py:889
  547.5 70.8 %copy-start.48 = (f32[256]{0:T(256)S(1)}, f32[256]{0:T(256)}, u32[]{:S(2)}) copy-start(f32[256]{0:T(256)} %param.34) | copy-start | bytes 3076
  547.5 71.8 %copy-start.41 = (f32[2,256]{1,0:T(2,128)S(1)}, f32[2,256]{1,0:T(2,128)}, u32[]{:S(2)}) copy-start(f32[2,256]{1,0:T(2,128)} %param.29) | copy-start | bytes 6148
  547.5 71.8 %copy-start.43 = (f32[2,256]{1,0:T(2,128)S(1)}, f32[2,256]{1,0:T(2,128)}, u32[]{:S(2)}) copy-start(f32[2,256]{1,0:T(2,128)} %param.28) | copy-start | bytes 6148
  547.5 72.4 %copy-start.37 = (f32[2,256,16]{1,2,0:T(8,128)S(1)}, f32[2,256,16]{1,2,0:T(8,128)}, u32[]{:S(2)}) copy-start(f32[2,256,16]{1,2,0:T(8,128)} %param.30) | copy-start | bytes 98308
  547.5 75.1 %copy-start.33 = (f32[2,256,128]{2,1,0:T(8,128)S(1)}, f32[2,256,128]{2,1,0:T(8,128)}, u32[]{:S(2)}) copy-start(f32[2,256,128]{2,1,0:T(8,128)} %param.26) | copy-start | bytes 786436
  547.5 75.1 %copy-start.34 = (f32[2,256,128]{2,1,0:T(8,128)S(1)}, f32[2,256,128]{2,1,0:T(8,128)}, u32[]{:S(2)}) copy-start(f32[2,256,128]{2,1,0:T(8,128)} %param.25) | copy-start | bytes 786436
  (39 other events, 665.3 us)
Sparse Core Ops, SparseCore 0:
  13.1 11.3 all-gather.22
  28.3 25.5 all-gather.24
  56.0 23.6 all-gather.26
  81.0 32.9 all-gather.28
  116.0 23.6 all-gather.30
  141.6 23.6 all-gather.32
  166.8 23.6 all-gather.34
  324.9 31.8 all-gather.38
  358.6 18.2 all-gather.40
  489.1 7.6 reduce-scatter.2
  499.7 9.0 reduce-scatter.4
  511.1 32.3 all-gather.42
  546.7 69.8 all-reduce.3
  618.3 57.7 all-gather.48
  677.7 101.8 all-gather.50
  781.3 57.5 all-gather.44
  840.6 101.9 all-gather.46
  944.8 285.5 all-gather.36
where the time goes:
time: 1270 us; the launch traced here: 1260 us
  Pallas kernels  548 us (43%)
  waiting for transfers between devices  493 us (39%)
  local copies, waits for them, and re-layouts  84.1 us (7%)
  other arithmetic  74.6 us (6%)
  blocking collectives  41.1 us (3%)
  between operations  16.2 us (1%)
    all_gather x1, waiting for transfers between devices, step(): new_head = lax.all_gather(quarter, 'rep', tiled=True)  199 us
    pallas_call x2, Pallas kernels, expert_dw(): pl.pallas_call(functools.partial(expert_dw_kernel, blk=blk, alias=alias),...  178 us
    all_gather x2, waiting for transfers between devices, step(): dys_all[l] = lax.all_gather(dys, both)  177 us
    pallas_call x2, Pallas kernels, moe_bwd(): pl.pallas_call(functools.partial(moe_bwd_kernel, rows=rows, blk=blk), out...  89.7 us
    pallas_call x1, Pallas kernels, head(): pl.pallas_call(functools.partial(head_kernel, tokens_all=tokens_all), out...  78.6 us
    pallas_call x2, Pallas kernels, moe_fwd(): pl.pallas_call(functools.partial(moe_fwd_kernel, rows=rows, blk=blk), out...  74.1 us
    all_gather x2, waiting for transfers between devices, step(): xs_all.append(lax.all_gather(xs, both))  47.9 us
    pallas_call x1, Pallas kernels, head_dw(): pl.pallas_call(functools.partial(head_dw_kernel, tokens_all=tokens_all),...  46.1 us
  transfers between devices with their start and end apart: 21, of which 9 were waited for; matrix products, arithmetic and copies ran while one was open for 9% of the time, Pallas kernels for 28%

commit v1 on v0

--- a/solution.py
+++ b/solution.py
@@ -19,9 +19,11 @@
 HEAD_PIECE = 512
 DW_PIECE = 384
 LSE_ROWS = 72
+KNOWN = 40960
 SUBLANES = 8
 NEG = -1e30
 ROW, COL = 0, 1
+LANES = 128
 
 
 def contract(a, b, ca, cb):
@@ -70,10 +72,6 @@
 
 def pair_of(x, axis):
     return jnp.split(x, 2, axis=axis)
-
-
-def side_by_side(ref):
-    return jnp.concatenate([ref[core].reshape(ref.shape[-2:]) for core in range(2)], axis=COL)
 
 
 def rms_stats(x):
@@ -105,8 +103,40 @@
     return dot(onehot, hi) + dot(onehot, mid) + dot(onehot, lo)
 
 
+def pieces(total, size):
+    edges = [*range(0, total, size), total]
+    return list(zip(edges, edges[1:]))
+
+
+def staggered(items, first, second):
+    held = None
+    for item in items:
+        made = first(item)
+        if held is not None:
+            second(*held)
+        held = (item, made)
+    second(*held)
+
+
+def own_first(x, mine):
+    lower, upper = pair_of(x, COL)
+    return jnp.where(mine == 0, x, jnp.concatenate([upper, lower], axis=COL))
+
+
+def sublane_groups(x):
+    return x.reshape(-1, SUBLANES, x.shape[COL])
+
+
+def both_cores(refs, lo, hi):
+    return jnp.concatenate([ref[lo:hi] for ref in refs], axis=COL)
+
+
 def params(vmem_mib, **kw):
     return pltpu.CompilerParams(vmem_limit_bytes=vmem_mib << 20, **kw)
+
+
+def cost(gflops, mbytes):
+    return pl.CostEstimate(flops=gflops * 10**9, bytes_accessed=mbytes * 10**6, transcendentals=0)
 
 
 def whole(shape):
@@ -118,55 +148,82 @@
     return [iota((rows, pos.shape[COL]), ROW) == pos for pos in pair_of(pos_row, ROW)]
 
 
-def moe_fwd_kernel(off, x_ref, gain_ref, wr_ref, prow_ref, pcol_ref, ecol_ref, wg_ref, wu_ref, wd_ref,
-                   out_ref, xs_out, y0_out, y1_out, xs_s, down_s, *, rows, blk):
+def expert_rows(off, expert, blk, body):
+    start = off[expert]
+    count = off[expert + 1] - start
+
+    def step(i, carry):
+        body(pl.multiple_of(start + i * blk, TILE))
+        return carry
+
+    lax.fori_loop(0, (count + blk - 1) // blk, step, 0)
+
+
+class ExpertWeights:
+    def __init__(self, refs, mine):
+        self.gate_refs, self.up_refs, down = refs[:2], refs[2:4], refs[4:]
+        self.half_ff = down[0].shape[2]
+        self.cores = [(pl.multiple_of(core * self.half_ff, TILE), ref) for core, ref in zip((mine, 1 - mine), down)]
+
+    def rows_of(self, core):
+        return pl.ds(core[0], self.half_ff)
+
+    def wide(self, refs, core):
+        return jnp.concatenate([ref[0, 0, self.rows_of(core)] for ref in refs], axis=COL)
+
+    def gate(self, core):
+        return self.wide(self.gate_refs, core)
+
+    def up(self, core):
+        return self.wide(self.up_refs, core)
+
+    def down(self, core):
+        return get(core[1]).reshape(self.half_ff, -1)
+
+
+def moe_fwd_kernel(off, fs, x_ref, gain_ref, wr_ref, prow_ref, pcol_ref, ecol_ref, *refs, rows, blk):
+    w_refs, (out_ref, xs_out, y0_out, y1_out, xs_s, down_s) = refs[:6], refs[6:]
     expert = pl.program_id(0)
-    toks = x_ref.shape[0]
+    toks = x_ref.shape[ROW]
+    weights = ExpertWeights(w_refs, fs[0])
 
     @pl.when(expert == 0)
     def _():
         normed = rms_norm(get(x_ref), get(gain_ref))
         hit0, hit1 = route_masks(get(prow_ref), rows)
-        spread = hot(hit0 | hit1)
-        xs = dot(spread, normed).astype(BF16)
+        xs = dot(hot(hit0 | hit1), normed).astype(BF16)
         put(xs_out, xs)
-        xs_s[pl.ds(0, rows), :] = xs
-        xs_s[pl.ds(rows, blk), :] = jnp.zeros((blk, xs.shape[1]), BF16)
+        xs_s[:rows] = own_first(xs, fs[0])
+        xs_s[rows:] = jnp.zeros((blk, xs.shape[COL]), BF16)
         fill(down_s, 0)
 
-    w_gate = side_by_side(wg_ref)
-    w_up = side_by_side(wu_ref)
-    w_down = get(wd_ref).reshape(w_gate.shape)
-    start = off[expert]
-    count = off[expert + 1] - start
-
-    def body(i, carry):
-        at = pl.multiple_of(start + i * blk, TILE)
-        xs = xs_s[pl.ds(at, blk), :]
-        gate = dot_nt(w_gate, xs)
-        up = dot_nt(w_up, xs)
-        hidden = (gate * jax.nn.sigmoid(gate) * up).astype(BF16)
-        down_s[pl.ds(at, blk), :] = dot_tn(hidden, w_down)
-        return carry
-
-    lax.fori_loop(0, (count + blk - 1) // blk, body, 0)
+    def body(at):
+        xs = xs_s[pl.ds(at, blk)]
+        out = down_s.at[pl.ds(at, blk)]
+
+        def hidden(core):
+            gate = dot_nt(weights.gate(core), xs)
+            return (gate * jax.nn.sigmoid(gate) * dot_nt(weights.up(core), xs)).astype(BF16)
+
+        downs = []
+        staggered(weights.cores, hidden, lambda core, made: downs.append(dot_tn(made, weights.down(core))))
+        put(out, functools.reduce(jnp.add, downs))
+
+    expert_rows(off, expert, blk, body)
 
     @pl.when(expert == pl.num_programs(0) - 1)
     def _():
         x = get(x_ref)
-        normed = rms_norm(x, get(gain_ref))
-        logits = dot_nt(normed, get(wr_ref))
-        gate0, gate1 = pair_gates(logits, get(ecol_ref), COL)
+        logits = dot_nt(rms_norm(x, get(gain_ref)), get(wr_ref))
+        gates = pair_gates(logits, get(ecol_ref), COL)
         col_id = iota((toks, rows), COL)
-        slot0, slot1 = pair_of(get(pcol_ref), COL)
-        pick0 = hot(col_id == slot0)
-        pick1 = hot(col_id == slot1)
         hi, mid, lo = split3(down_s[:rows])
-        y0 = dot(pick0, hi) + dot(pick0, mid) + dot(pick0, lo)
-        y1 = dot(pick1, hi) + dot(pick1, mid) + dot(pick1, lo)
-        put(y0_out, y0)
-        put(y1_out, y1)
-        put(out_ref, x + (y0 * gate0 + y1 * gate1))
+        for slot, gate, y_out in zip(pair_of(get(pcol_ref), COL), gates, (y0_out, y1_out)):
+            pick = hot(col_id == slot)
+            y = dot(pick, hi) + dot(pick, mid) + dot(pick, lo)
+            put(y_out, y)
+            x = x + y * gate
+        put(out_ref, x)
 
 
 def pair_gates(logits, experts, axis):
@@ -178,46 +235,47 @@
     return e0 / (e0 + e1), e1 / (e0 + e1)
 
 
-def moe_bwd_kernel(off, dx_ref, x_ref, gain_ref, wr_ref, prow_ref, pcol_ref, erow_ref, ecol_ref, y0_ref, y1_ref, xs_ref,
-                   wg_ref, wu_ref, wd_ref, dx_out, dys_out, dwr_out, dg_out, xs_s, dys_s, dxs_s, *, rows, blk):
+def moe_bwd_kernel(off, fs, dx_ref, x_ref, gain_ref, wr_ref, prow_ref, pcol_ref, erow_ref, ecol_ref, y0_ref, y1_ref, xs_ref, *refs, rows, blk):
+    w_refs, (dx_out, dys_out, dwr_out, dg_out, xs_s, dys_s, dxs_s) = refs[:6], refs[6:]
     expert = pl.program_id(0)
     toks, width = x_ref.shape
+    mine = fs[0]
+    weights = ExpertWeights(w_refs, mine)
 
     @pl.when(expert == 0)
     def _():
-        dx = get(dx_ref)
         normed = rms_norm(get(x_ref), get(gain_ref))
-        logits_t = dot_nt(get(wr_ref), normed)
-        gate0, gate1 = pair_gates(logits_t, get(erow_ref), ROW)
+        gate0, gate1 = pair_gates(dot_nt(get(wr_ref), normed), get(erow_ref), ROW)
         hit0, hit1 = route_masks(get(prow_ref), rows)
-        spread = hot(hit0 | hit1)
         gate_rows = axis_sum(keep(hit0, gate0) + keep(hit1, gate1), COL)
-        dys = select_rows(spread, dx) * gate_rows
+        dys = select_rows(hot(hit0 | hit1), get(dx_ref)) * gate_rows
         put(dys_out, dys)
-        dys_s[pl.ds(0, rows), :] = dys.astype(BF16)
-        dys_s[pl.ds(rows, blk), :] = jnp.zeros((blk, width), BF16)
-        xs_s[pl.ds(0, rows), :] = get(xs_ref)
-        xs_s[pl.ds(rows, blk), :] = jnp.zeros((blk, width), BF16)
+        tail = jnp.zeros((blk, width), BF16)
+        dys_s[:rows] = dys.astype(BF16)
+        dys_s[rows:] = tail
+        xs_s[:rows] = own_first(get(xs_ref), mine)
+        xs_s[rows:] = tail
         fill(dxs_s, 0)
 
-    w_gate = side_by_side(wg_ref)
-    w_up = side_by_side(wu_ref)
-    w_down = get(wd_ref).reshape(w_gate.shape)
-    start = off[expert]
-    count = off[expert + 1] - start
-
-    def body(i, carry):
-        at = pl.multiple_of(start + i * blk, TILE)
-        xs = xs_s[pl.ds(at, blk), :]
-        dys = dys_s[pl.ds(at, blk), :]
-        gate = dot_nt(w_gate, xs)
-        up = dot_nt(w_up, xs)
-        d_hidden = dot_nt(w_down, dys)
-        d_gate, d_up, _ = glu_bwd(gate, up, d_hidden)
-        dxs_s[pl.ds(at, blk), :] = dot_tn(d_gate, w_gate) + dot_tn(d_up, w_up)
-        return carry
-
-    lax.fori_loop(0, (count + blk - 1) // blk, body, 0)
+    def body(at):
+        xs = xs_s[pl.ds(at, blk)]
+        dys = dys_s[pl.ds(at, blk)]
+
+        def gradients(core):
+            gate = dot_nt(weights.gate(core), xs)
+            up = dot_nt(weights.up(core), xs)
+            return glu_bwd(gate, up, dot_nt(weights.down(core), dys))
+
+        parts = []
+
+        def back(core, made):
+            d_gate, d_up, _ = made
+            parts.extend([dot_tn(d_gate, weights.gate(core)), dot_tn(d_up, weights.up(core))])
+
+        staggered(weights.cores, gradients, back)
+        dxs_s[pl.ds(at, blk)] = functools.reduce(jnp.add, parts)
+
+    expert_rows(off, expert, blk, body)
 
     @pl.when(expert == pl.num_programs(0) - 1)
     def _():
@@ -237,8 +295,7 @@
         put(dwr_out, dot_tn(d_logits, normed))
         col_id = iota((toks, rows), COL)
         slot0, slot1 = pair_of(get(pcol_ref), COL)
-        collect = hot((col_id == slot0) | (col_id == slot1))
-        d_normed = select_rows(collect, dxs_s[pl.ds(0, rows), :]) + dot(d_logits, get(wr_ref))
+        d_normed = own_first(select_rows(hot((col_id == slot0) | (col_id == slot1)), dxs_s[:rows]), mine) + dot(d_logits, get(wr_ref))
         d_x, d_gain = rms_norm_bwd(x, gain, d_normed.astype(BF16).astype(F32))
         put(dx_out, dx + d_x)
         put(dg_out, d_gain)
@@ -249,92 +306,78 @@
     act = gate * sig
     d_gate = (d_hidden * up * (sig + act * (1.0 - sig))).astype(BF16)
     d_up = (d_hidden * act).astype(BF16)
-    return d_gate, d_up, act
-
-
-def expert_specs(ff, half):
-    up_spec = pl.BlockSpec((2, 1, ff, half), lambda e, *_: (0, e, 0, 0))
-    down_spec = pl.BlockSpec((2, 1, ff // 2, 2 * half), lambda e, *_: (0, e, 0, 0))
-    return [up_spec, up_spec, down_spec]
-
-
-def moe_fwd(off, x, gain, w_r, pos_row, pos_col, exp_col, w_gate, w_up, w_down, rows):
+    return d_gate, d_up, (act * up).astype(BF16)
+
+
+def expert_specs(layer, weights):
+    return [pl.BlockSpec((1, 1, *w.shape[2:]), lambda e, *_: (layer, e, 0, 0)) for w in weights]
+
+
+def moe_fwd(layer, off, fs, x, gain, w_r, pos_row, pos_col, exp_col, weights, rows):
     toks, width = x.shape
-    experts, ff = w_gate.shape[1], w_gate.shape[2]
-    blk = 128
+    blk = LANES
     tok_out = jax.ShapeDtypeStruct((toks, width), F32)
+    out_shapes = (tok_out, jax.ShapeDtypeStruct((rows, width), BF16), tok_out, tok_out)
     small = [x, gain, w_r, pos_row, pos_col, exp_col]
     return pl.pallas_call(
         functools.partial(moe_fwd_kernel, rows=rows, blk=blk),
-        out_shape=(tok_out, jax.ShapeDtypeStruct((rows, width), BF16), tok_out, tok_out),
+        out_shape=out_shapes,
         grid_spec=pltpu.PrefetchScalarGridSpec(
-            num_scalar_prefetch=1,
-            grid=(experts,),
-            in_specs=[whole(a.shape) for a in small] + expert_specs(ff, width // 2),
-            out_specs=(whole((toks, width)), whole((rows, width)), whole((toks, width)), whole((toks, width))),
+            num_scalar_prefetch=2,
+            grid=(w_r.shape[ROW],),
+            in_specs=[whole(a.shape) for a in small] + expert_specs(layer, weights),
+            out_specs=tuple(whole(s.shape) for s in out_shapes),
             scratch_shapes=[pltpu.VMEM((rows + blk, width), BF16), pltpu.VMEM((rows + blk, width), F32)],
         ),
         compiler_params=params(48),
-        cost_estimate=pl.CostEstimate(flops=30_000_000_000, bytes_accessed=45_000_000, transcendentals=0),
+        cost_estimate=cost(30, 45),
         name="moe_fwd",
-    )(off, *small, w_gate, w_up, w_down)
-
-
-def moe_bwd(off, dx, x, gain, w_r, pos_row, pos_col, exp_row, exp_col, y0, y1, xs, w_gate, w_up, w_down, rows):
+    )(off, fs, *small, *weights)
+
+
+def moe_bwd(layer, off, fs, dx, x, gain, w_r, pos_row, pos_col, exp_row, exp_col, y0, y1, xs, weights, rows):
     toks, width = x.shape
-    experts, ff = w_gate.shape[1], w_gate.shape[2]
-    blk = 128
+    blk = LANES
     small = [dx, x, gain, w_r, pos_row, pos_col, exp_row, exp_col, y0, y1, xs]
-    out_shapes = (
-        jax.ShapeDtypeStruct((toks, width), F32),
-        jax.ShapeDtypeStruct((rows, width), F32),
-        jax.ShapeDtypeStruct((experts, width), F32),
-        jax.ShapeDtypeStruct((1, width), F32),
-    )
+    out_shapes = tuple(jax.ShapeDtypeStruct((count, width), F32) for count in (toks, rows, w_r.shape[ROW], 1))
+    buffer = pltpu.VMEM((rows + blk, width), BF16)
     return pl.pallas_call(
         functools.partial(moe_bwd_kernel, rows=rows, blk=blk),
         out_shape=out_shapes,
         grid_spec=pltpu.PrefetchScalarGridSpec(
-            num_scalar_prefetch=1,
-            grid=(experts,),
-            in_specs=[whole(a.shape) for a in small] + expert_specs(ff, width // 2),
+            num_scalar_prefetch=2,
+            grid=(w_r.shape[ROW],),
+            in_specs=[whole(a.shape) for a in small] + expert_specs(layer, weights),
             out_specs=tuple(whole(s.shape) for s in out_shapes),
-            scratch_shapes=[
-                pltpu.VMEM((rows + blk, width), BF16),
-                pltpu.VMEM((rows + blk, width), BF16),
-                pltpu.VMEM((rows + blk, width), F32),
-            ],
+            scratch_shapes=[buffer, buffer, pltpu.VMEM((rows + blk, width), F32)],
         ),
         compiler_params=params(60),
-        cost_estimate=pl.CostEstimate(flops=50_000_000_000, bytes_accessed=50_000_000, transcendentals=0),
+        cost_estimate=cost(50, 50),
         name="moe_bwd",
-    )(off, *small, w_gate, w_up, w_down)
-
-
-def expert_dw_kernel(off, fs, lr_ref, xs_hbm, dys_hbm, wg_ref, wu_ref, wd_ref, mg_ref, mu_ref, md_ref, *refs, blk, alias):
-    refs = refs[3:] if alias else refs
-    og_ref, ou_ref, od_ref, xbuf, dbuf, sems, acc_g, acc_u, acc_d = refs
+    )(off, fs, *small, *weights)
+
+
+def expert_dw_kernel(off, fs, lr_ref, xs_hbm, dys_hbm, *refs, blk, alias):
+    w_refs, masters, refs = refs[:6], refs[6:9], refs[12 if alias else 9 :]
+    outs, (xbuf, dbuf, sems), accs = refs[:3], refs[3:6], refs[6:]
+    acc_g, acc_u, acc_d = accs
     expert = pl.program_id(0)
-    experts = pl.num_programs(0)
     seqs = xs_hbm.shape[0]
-    ff, half = acc_g.shape
+    half = acc_g.shape[COL]
     mine = fs[0]
-
-    def copies(e, slot, go):
+    weights = ExpertWeights(w_refs, mine)
+
+    def copies(e, slot, act):
         at = 0
         for s in range(seqs):
             start = pl.multiple_of(off[s, e], TILE)
             count = pl.multiple_of(off[s, e + 1] - off[s, e], TILE)
-            dst = pl.multiple_of(at, TILE)
+            target = pl.ds(pl.multiple_of(at, TILE), count)
 
             @pl.when(count > 0)
             def _():
-                for hbm, buf, k in ((xs_hbm, xbuf, 0), (dys_hbm, dbuf, 1)):
-                    copy = pltpu.make_async_copy(hbm.at[s, pl.ds(start, count), :], buf.at[slot, pl.ds(dst, count), :], sems.at[slot, k])
-                    if go:
-                        copy.start()
-                    else:
-                        copy.wait()
+                for k, (hbm, buf) in enumerate(((xs_hbm, xbuf), (dys_hbm, dbuf))):
+                    act(pltpu.make_async_copy(hbm.at[s, pl.ds(start, count)], buf.at[slot, target], sems.at[slot, k]))
 
             at = at + count
         return at
@@ -343,105 +386,74 @@
 
     @pl.when(expert == 0)
     def _():
-        copies(0, 0, True)
-
-    @pl.when(expert + 1 < experts)
-    def _():
-        copies(expert + 1, 1 - slot, True)
-
-    total = pl.multiple_of(copies(expert, slot, False), TILE)
-    xbuf[slot, pl.ds(total, blk), :] = jnp.zeros((blk, xbuf.shape[2]), BF16)
-    dbuf[slot, pl.ds(total, blk), :] = jnp.zeros((blk, dbuf.shape[2]), F32)
-    fill(acc_g, 0)
-    fill(acc_u, 0)
-    fill(acc_d, 0)
-    w_gate = side_by_side(wg_ref)
-    w_up = side_by_side(wu_ref)
-    w_down = get(wd_ref).reshape(w_gate.shape)
+        copies(0, 0, lambda copy: copy.start())
+
+    @pl.when(expert + 1 < pl.num_programs(0))
+    def _():
+        copies(expert + 1, 1 - slot, lambda copy: copy.start())
+
+    total = pl.multiple_of(copies(expert, slot, lambda copy: copy.wait()), TILE)
+    for buf in (xbuf, dbuf):
+        buf[slot, pl.ds(total, blk)] = jnp.zeros((blk, buf.shape[2]), buf.dtype)
+    for acc in accs:
+        fill(acc, 0)
 
     def body(i, carry):
-        at = pl.multiple_of(i * blk, blk)
-        xs = xbuf[slot, pl.ds(at, blk), :]
-        own = xbuf[slot, pl.ds(at, blk), pl.ds(pl.multiple_of(mine * half, half), half)]
-        dys = dbuf[slot, pl.ds(at, blk), :].astype(BF16)
-        gate = dot_nt(w_gate, xs)
-        up = dot_nt(w_up, xs)
-        d_hidden = dot_nt(w_down, dys)
-        d_gate, d_up, act = glu_bwd(gate, up, d_hidden)
-        hidden = (act * up).astype(BF16)
-        put(acc_g, get(acc_g) + dot(d_gate, own))
-        put(acc_u, get(acc_u) + dot(d_up, own))
-        hidden_own = jnp.where(mine == 0, hidden[: ff // 2], hidden[ff // 2 :])
-        put(acc_d, get(acc_d) + dot(hidden_own, dys))
+        rows = pl.ds(pl.multiple_of(i * blk, blk), blk)
+        xs = own_first(xbuf[slot, rows], mine)
+        dys = dbuf[slot, rows].astype(BF16)
+        own, xs_t, dys_t = xs[:, :half], xs.T, dys.T
+
+        def gradients(core):
+            return glu_bwd(dot(weights.gate(core), xs_t), dot(weights.up(core), xs_t), dot(weights.down(core), dys_t))
+
+        def add(core, made):
+            d_gate, d_up, hidden = made
+            part = weights.rows_of(core)
+            acc_g[part] += dot(d_gate, own)
+            acc_u[part] += dot(d_up, own)
+            if core is weights.cores[0]:
+                put(acc_d, get(acc_d) + dot(hidden, dys))
+
+        staggered(weights.cores, gradients, add)
         return carry
 
     lax.fori_loop(0, (total + blk - 1) // blk, body, 0)
-    for out, master, acc in ((og_ref, mg_ref, acc_g), (ou_ref, mu_ref, acc_u), (od_ref, md_ref, acc_d)):
+    for out, master, acc in zip(outs, masters, accs):
         put(out, get(master) - get(lr_ref) * get(acc).reshape(out.shape))
 
 
-def expert_dw(layer, off, fs, lr, xs, dys, w_gate, w_up, w_down, m_gate, m_up, m_down, prev):
+def expert_dw(layer, off, fs, lr, xs, dys, weights, masters, prev):
     seqs, _, width = xs.shape
-    _, experts, ff, half = m_gate.shape
-    blk = 256
-    most = seqs * ((width + TILE - 1) // TILE * TILE)
+    experts = masters[0].shape[1]
+    blk = 2 * LANES
+    most = seqs * width + blk
     any_spec = pl.BlockSpec(memory_space=pl.ANY)
-    up_master = pl.BlockSpec((1, 1, ff, half), lambda e, *_: (layer, e, 0, 0))
-    down_master = pl.BlockSpec((1, 1, ff // 2, width), lambda e, *_: (layer, e, 0, 0))
-    masters = [up_master, up_master, down_master]
+    specs = expert_specs(layer, masters)
     alias = prev is not None
-    in_specs = [whole(lr.shape), any_spec, any_spec] + expert_specs(ff, half) + masters
+    in_specs = [whole(lr.shape), any_spec, any_spec] + expert_specs(layer, weights) + specs
     in_specs += [any_spec] * 3 if alias else []
+    first_prev = len(in_specs) - 1
     return pl.pallas_call(
         functools.partial(expert_dw_kernel, blk=blk, alias=alias),
-        out_shape=tuple(jax.ShapeDtypeStruct(m.shape, F32) for m in (m_gate, m_up, m_down)),
+        out_shape=tuple(jax.ShapeDtypeStruct(m.shape, F32) for m in masters),
         grid_spec=pltpu.PrefetchScalarGridSpec(
             num_scalar_prefetch=2,
             grid=(experts,),
             in_specs=in_specs,
-            out_specs=tuple(masters),
+            out_specs=tuple(specs),
             scratch_shapes=[
-                pltpu.VMEM((2, most + blk, width), BF16),
-                pltpu.VMEM((2, most + blk, width), F32),
+                pltpu.VMEM((2, most, width), BF16),
+                pltpu.VMEM((2, most, width), F32),
                 pltpu.SemaphoreType.DMA((2, 2)),
-                pltpu.VMEM((ff, half), F32),
-                pltpu.VMEM((ff, half), F32),
-                pltpu.VMEM((ff // 2, width), F32),
-            ],
+            ]
+            + [pltpu.VMEM(m.shape[2:], F32) for m in masters],
         ),
-        input_output_aliases={11: 0, 12: 1, 13: 2} if alias else {},
+        input_output_aliases={first_prev + k: k for k in range(3)} if alias else {},
         compiler_params=params(62),
-        cost_estimate=pl.CostEstimate(flops=90_000_000_000, bytes_accessed=150_000_000, transcendentals=0),
+        cost_estimate=cost(60, 150),
         name="expert_dw",
-    )(off, fs, lr, xs, dys, w_gate, w_up, w_down, m_gate, m_up, m_down, *(prev or ()))
-
-
-def pieces(total, size):
-    edges = [*range(0, total, size), total]
-    return list(zip(edges, edges[1:]))
-
-
-def staggered(items, first, second):
-    held = None
-    for item in items:
-        made = first(item)
-        if held is not None:
-            second(*held)
-        held = (item, made)
-    second(*held)
-
-
-def own_first(x, mine):
-    lower, upper = pair_of(x, COL)
-    return jnp.where(mine == 0, x, jnp.concatenate([upper, lower], axis=COL))
-
-
-def sublane_groups(x):
-    return x.reshape(-1, SUBLANES, x.shape[COL])
-
-
-def both_cores(refs, lo, hi):
-    return jnp.concatenate([ref[lo:hi] for ref in refs], axis=COL)
+    )(off, fs, lr, xs, dys, *weights, *masters, *(prev or ()))
 
 
 def head_kernel(fs, x_ref, gain_ref, lab_ref, wa_ref, wb_ref, fin_out, lse_out, dx_out, dg_out, loss_out, fin_s, top_s, sum_s, pick_s, acc_s, *, tokens_all):
@@ -530,30 +542,30 @@
             scratch_shapes=[pltpu.VMEM((width, toks), BF16)] + [pltpu.VMEM((SUBLANES, toks), F32)] * 3 + [pltpu.VMEM((toks, width), F32)],
         ),
         compiler_params=params(56),
-        cost_estimate=pl.CostEstimate(flops=55_000_000_000, bytes_accessed=70_000_000, transcendentals=0),
+        cost_estimate=cost(55, 70),
         name="head_own",
     )(fs, *small, w_own, w_other)
 
 
-def head_dw_kernel(fs, fin_ref, lse_ref, lab_ref, wa_ref, wb_ref, own_out, oth_out, fin_s, fin_t, *, tokens_all):
+def head_dw_kernel(fs, lr_ref, fin_ref, lse_ref, lab_ref, wa_ref, wb_ref, m_ref, new_out, oth_out, fin_s, fin_t, acc_s, *, tokens_all):
     tile, half = wa_ref.shape
     seqs = fin_s.shape[0]
     mine = fs[0]
-    base = (fs[1] * pl.num_programs(0) + pl.program_id(0)) * tile
+    base = (mine * pl.num_programs(0) + pl.program_id(0)) * tile
     parts = pieces(tile, DW_PIECE)
-    fill(own_out, 0)
+    fill(acc_s, 0)
     fill(oth_out, 0)
 
     @pl.when(pl.program_id(0) == 0)
     def _():
         for s in range(seqs):
-            fin = own_first(fin_ref[mine * seqs + s], mine)
+            fin = own_first(fin_ref[s], mine)
             fin_s[s] = fin
             fin_t[s] = fin.T
 
     def body(s, carry):
-        lse = lse_ref[mine * seqs + s, :1] + jnp.log2(jnp.float32(tokens_all))
-        lab = lab_ref[mine * seqs + s] - base
+        lse = lse_ref[s, :1] + jnp.log2(jnp.float32(tokens_all))
+        lab = lab_ref[s] - base
 
         def gradient(part):
             logits = dot(both_cores((wa_ref, wb_ref), *part), fin_t[s]) * LOG2E
@@ -562,61 +574,66 @@
 
         def add_gradient(part, grad):
             rows = slice(*part)
-            own_out[rows] += dot(grad, fin_s[s, :, :half])
+            acc_s[rows] += dot(grad, fin_s[s, :, :half])
             oth_out[rows] += dot(grad, fin_s[s, :, half:])
 
         staggered(parts, gradient, add_gradient)
         return carry
 
     lax.fori_loop(0, seqs, body, 0)
-
-
-def head_dw(fs, fin, lse, labels, w_own, w_other, tokens_all):
+    put(new_out, get(m_ref) - get(lr_ref) * get(acc_s))
+
+
+def head_dw(fs, lr, fin, lse, labels, w_own, w_other, master, tokens_all):
     seqs, toks, width = fin.shape
-    vocab, half = w_own.shape
+    vocab, half = master.shape
+    steps = HEAD_STEPS // 2
     tile = vocab // HEAD_STEPS
-    steps = HEAD_STEPS // (seqs // 2)
-    out = jax.ShapeDtypeStruct((steps * tile, half), F32)
-    out_spec = pl.BlockSpec((tile, half), lambda i, *_: (i, 0))
-    w_spec = pl.BlockSpec((tile, half), lambda i, f: (f[1] * steps + i, 0))
+    spec = pl.BlockSpec((tile, half), lambda i, f: (f[0] * steps + i, 0))
+    small = [lr, fin, lse, labels]
     return pl.pallas_call(
         functools.partial(head_dw_kernel, tokens_all=tokens_all),
-        out_shape=(out, out),
+        out_shape=(jax.ShapeDtypeStruct((vocab, half), F32), jax.ShapeDtypeStruct((steps * tile, half), F32)),
         grid_spec=pltpu.PrefetchScalarGridSpec(
             num_scalar_prefetch=1,
             grid=(steps,),
-            in_specs=[whole(fin.shape), whole(lse.shape), whole(labels.shape), w_spec, w_spec],
-            out_specs=(out_spec, out_spec),
-            scratch_shapes=[pltpu.VMEM((seqs // 2, toks, width), BF16), pltpu.VMEM((seqs // 2, width, toks), BF16)],
+            in_specs=[whole(a.shape) for a in small] + [spec] * 3,
+            out_specs=(spec, pl.BlockSpec((tile, half), lambda i, *_: (i, 0))),
+            scratch_shapes=[
+                pltpu.VMEM((seqs, toks, width), BF16),
+                pltpu.VMEM((seqs, width, toks), BF16),
+                pltpu.VMEM((tile, half), F32),
+            ],
         ),
-        compiler_params=params(56),
-        cost_estimate=pl.CostEstimate(flops=40_000_000_000, bytes_accessed=40_000_000, transcendentals=0),
+        compiler_params=params(60),
+        cost_estimate=cost(140, 70),
         name="head_dw",
-    )(fs, fin, lse, labels, w_own, w_other)
-
-
-def head_upd_kernel(fs, lr_ref, own_ref, recv_ref, m_ref, new_out):
-    put(new_out, get(m_ref) - get(lr_ref) * (get(own_ref) + get(recv_ref)))
-
-
-def head_upd(fs, lr, own, received, master):
-    rows, half = own.shape
-    tile = master.shape[ROW] // HEAD_STEPS
-    steps = rows // tile
-    spec = pl.BlockSpec((tile, half), lambda i, *_: (i, 0))
+    )(fs, *small, w_own, w_other, master)
+
+
+def head_upd_kernel(fs, lr_ref, grad_ref, m_ref, prev_ref, new_out):
+    put(new_out, get(m_ref) - get(lr_ref) * get(grad_ref))
+
+
+def head_upd(fs, lr, grad, master, prev):
+    vocab, half = master.shape
+    steps = HEAD_STEPS // 2
+    tile = vocab // HEAD_STEPS
+    spec = pl.BlockSpec((tile, half), lambda i, f: ((1 - f[0]) * steps + i, 0))
     return pl.pallas_call(
         head_upd_kernel,
-        out_shape=jax.ShapeDtypeStruct((rows, half), F32),
+        out_shape=jax.ShapeDtypeStruct((vocab, half), F32),
         grid_spec=pltpu.PrefetchScalarGridSpec(
             num_scalar_prefetch=1,
             grid=(steps,),
-            in_specs=[whole(lr.shape), spec, spec, pl.BlockSpec((tile, half), lambda i, f: (f[1] * steps + i, 0))],
+            in_specs=[whole(lr.shape), pl.BlockSpec((tile, half), lambda i, *_: (i, 0)), spec, pl.BlockSpec(memory_space=pl.ANY)],
             out_specs=spec,
         ),
+        input_output_aliases={4: 0},
         compiler_params=params(48),
-        cost_estimate=pl.CostEstimate(flops=8_000_000_000, bytes_accessed=33_000_000, transcendentals=0),
+        cost_estimate=cost(15, 50),
         name="head_upd",
-    )(fs, lr, own, received, master)
+    )(fs, lr, grad, master, prev)
 
 
 def embed_upd_kernel(bounds, keys, perm, lr_ref, rows_ref, m_ref, new_out, wide_s):
@@ -654,7 +671,7 @@
             scratch_shapes=[pltpu.VMEM(grads.shape, F32)],
         ),
         compiler_params=params(48),
-        cost_estimate=pl.CostEstimate(flops=25_000_000_000, bytes_accessed=66_000_000, transcendentals=0),
+        cost_estimate=cost(25, 66),
         name="embed_upd",
     )(bounds, keys, perm, lr, grads, master)
 
@@ -752,7 +769,7 @@
         in_specs=attn_specs(small, w_all, layer),
         out_specs=whole(x.shape),
         compiler_params=params(48),
-        cost_estimate=pl.CostEstimate(flops=8_000_000_000, bytes_accessed=5_000_000, transcendentals=0),
+        cost_estimate=cost(8, 5),
         name="attn_fwd",
     )(*small, w_all)
 
@@ -769,7 +786,7 @@
         in_specs=attn_specs(small, w_all, layer),
         out_specs=(whole(x.shape), whole(grads.shape)),
         compiler_params=params(60),
-        cost_estimate=pl.CostEstimate(flops=15_000_000_000, bytes_accessed=10_000_000, transcendentals=0),
+        cost_estimate=cost(15, 10),
         name="attn_bwd",
     )(*small, w_all)
 
@@ -825,7 +842,7 @@
         misc = misc.astype(BF16).astype(F32).reshape(-1)
         packed = jnp.concatenate([misc, ints])
         n_misc = misc.shape[0]
-        packed = jnp.pad(packed, (0, -packed.shape[0] % 1024)).reshape(-1, 128)
+        packed = jnp.pad(packed, (0, KNOWN - packed.shape[0])).reshape(-1, LANES)
         known = lax.all_gather(packed, both).reshape(device_count, -1)
         two = lax.dynamic_slice_in_dim(known, pair * 2, 2, 0)[:, :n_misc].reshape(2, -1, half)
         misc_all = jnp.concatenate([two[0], two[1]], axis=1)
@@ -842,12 +859,12 @@
         attn_pack = jnp.concatenate([w_query, w_key, w_value, w_attn_out], axis=2).astype(BF16)
         attn_all = lax.all_gather(attn_pack, 'fsdp')
 
-        def gather(x):
-            return lax.all_gather(x.astype(BF16), 'fsdp')
-
-        expert_w = [(gather(m_gate[l]), gather(m_up[l]), gather(w_down[l])) for l in range(layers)]
-        head_w = (m_head.astype(BF16),)
-        head_w += (lax.ppermute(head_w[0], 'fsdp', swap),)
+        def with_partner(x):
+            rounded = x.astype(BF16)
+            return rounded, lax.ppermute(rounded, 'fsdp', swap)
+
+        expert_w = with_partner(m_gate) + with_partner(m_up) + with_partner(w_down)
+        head_w = with_partner(m_head)
 
         partner_ids = lax.dynamic_index_in_dim(ids_all, pair * 2 + 1 - me, 0, keepdims=False)
         wanted = jnp.concatenate([tok_ids[0], partner_ids]) - me * vocab_share
@@ -863,7 +880,7 @@
         for l in range(layers):
             mid = attn_fwd(l, x, gain_attn[l], *tables, attn_all, *widths)
             pos, start = placed[l]
-            out, xs, y0, y1 = moe_fwd(start, mid, gain_mlp[l], w_r[l], pos.T, pos, experts_of[l], *expert_w[l], rows)
+            out, xs, y0, y1 = moe_fwd(l, start, fs, mid, gain_mlp[l], w_r[l], pos.T, pos, experts_of[l], expert_w, rows)
             kept.append((x, mid, xs, y0, y1))
             xs_all.append(lax.all_gather(xs, both))
             x = out
@@ -874,27 +891,24 @@
 
         dys_all = [None] * layers
         reduced = [None] * layers
-        new_head = None
         for l in reversed(range(layers)):
             x, mid, xs, y0, y1 = kept[l]
             pos, start = placed[l]
-            dx, dys, d_router, d_mlp = moe_bwd(start, dx, mid, gain_mlp[l], w_r[l], pos.T, pos, experts_of[l].T, experts_of[l], y0, y1, xs, *expert_w[l], rows)
+            dx, dys, d_router, d_mlp = moe_bwd(l, start, fs, dx, mid, gain_mlp[l], w_r[l], pos.T, pos, experts_of[l].T, experts_of[l], y0, y1, xs, expert_w, rows)
             dys_all[l] = lax.all_gather(dys, both)
-            if new_head is None:
-                fin_all, _ = lax.optimization_barrier((fin_all, dx))
-                own_grad, other_grad = head_dw(fs, fin_all, lse_all, labels_all[:, None], *head_w, tokens_all)
-                dx, _ = lax.optimization_barrier((dx, own_grad))
             dx, grads = attn_bwd(l, dx, x, gain_attn[l], *tables, d_router, d_mlp, d_final, loss, attn_all, *widths)
-            if new_head is None:
-                quarter = head_upd(fs, lr, own_grad, lax.ppermute(other_grad, 'fsdp', swap), m_head)
-                new_head = lax.all_gather(quarter, 'rep', tiled=True)
             reduced[l] = lax.psum(lax.psum_scatter(grads, 'fsdp', scatter_dimension=0, tiled=False), 'rep')
 
         d_rows = lax.all_gather(dx.astype(BF16), both).reshape(tokens_all, width)
 
+        fin_all, _ = lax.optimization_barrier((fin_all, dx))
+        new_head, other_grad = head_dw(fs, lr, fin_all, lse_all, labels_all[:, None], *head_w, m_head, tokens_all)
+        other_grad = lax.ppermute(other_grad, 'fsdp', swap)
         new_experts = None
         for l in reversed(range(layers)):
-            new_experts = expert_dw(l, starts_all[:, l], fs, lr, xs_all[l], dys_all[l], *expert_w[l], m_gate, m_up, w_down, new_experts)
+            new_experts = expert_dw(l, starts_all[:, l], fs, lr, xs_all[l], dys_all[l], expert_w, (m_gate, m_up, w_down), new_experts)
+
+        new_head = head_upd(fs, lr, other_grad, m_head, new_head)
 
         block = 1336
         local_id = ids_all.reshape(-1) - me * vocab_share

time: 1270 us -> 952 us (0.75)
  waiting for transfers between devices: 493 us -> 202 us
  Pallas kernels: 548 us -> 609 us
  blocking collectives: 41.1 us -> 0 us
  local copies, waits for them, and re-layouts: 84.1 us -> 44.7 us
    all_gather x7 -> x1, waiting for transfers between devices: 199 us -> 16 us  [step(): known = lax.all_gather(packed, both).reshape(device_count, -1)]
    pallas_call x1, Pallas kernels: 46.1 us -> 164 us  [head_dw(): pl.pallas_call(functools.partial(head_dw_kernel, tokens_all=tokens_all),...]
    all_gather x2, waiting for transfers between devices: 177 us -> 114 us  [step(): dys_all[l] = lax.all_gather(dys, both)]
    all_gather x2, waiting for transfers between devices: 47.9 us -> 0.02 us  [step(): xs_all.append(lax.all_gather(xs, both))]
    all_gather x1 -> x0, blocking collectives: 41.1 us -> none  [step(): known = lax.all_gather(packed, both).reshape(device_count, -1)]
    another operation x8 -> x5, other arithmetic: 31.4 us -> 0.02 us
    convert_element_type x1 -> x4, other arithmetic: 20.6 us -> 51.9 us  [with_partner(): rounded = x.astype(BF16)]
    pallas_call x2, Pallas kernels: 178 us -> 147 us  [expert_dw(): pl.pallas_call(functools.partial(expert_dw_kernel, blk=blk, alias=alias),...]
  transfers between devices with their start and end apart: 21 -> 18, of which waited for: 9 -> 7; matrix products, arithmetic and copies ran while one was open for 9% -> 10% of each run, Pallas kernels for 28% -> 38%
where the time goes in v1:
time: 952 us; the launch traced here: 945 us
  Pallas kernels  609 us (64%)
  waiting for transfers between devices  202 us (21%)
  other arithmetic  70.8 us (7%)
  local copies, waits for them, and re-layouts  44.7 us (5%)
  between operations  16.2 us (2%)
    pallas_call x1, Pallas kernels, head_dw(): pl.pallas_call(functools.partial(head_dw_kernel, tokens_all=tokens_all),...  164 us
    pallas_call x2, Pallas kernels, expert_dw(): pl.pallas_call(functools.partial(expert_dw_kernel, blk=blk, alias=alias),...  147 us
    all_gather x2, waiting for transfers between devices, step(): dys_all[l] = lax.all_gather(dys, both)  114 us
    pallas_call x1, Pallas kernels, head(): pl.pallas_call(functools.partial(head_kernel, tokens_all=tokens_all), out...  78.8 us
    pallas_call x2, Pallas kernels, moe_bwd(): pl.pallas_call(functools.partial(moe_bwd_kernel, rows=rows, blk=blk), out...  74.4 us
    pallas_call x2, Pallas kernels, moe_fwd(): pl.pallas_call(functools.partial(moe_fwd_kernel, rows=rows, blk=blk), out...  59.5 us
    convert_element_type x4, other arithmetic, with_partner(): rounded = x.astype(BF16)  51.9 us
    pallas_call x1, Pallas kernels, embed_upd(): pl.pallas_call(embed_upd_kernel, out_shape=jax.ShapeDtypeStruct((vocab, w...  38.8 us
  transfers between devices with their start and end apart: 18, of which 7 were waited for; matrix products, arithmetic and copies ran while one was open for 10% of the time, Pallas kernels for 38%

profile of v1, /device:TPU:0, one launch (start us, length us, event | category | flops | bytes accessed | tf_op | source)
XLA Modules:
  0.0 945.5 jit_solution(12084717065499015369)
XLA Ops:
  7.2 13.5 %bitcast_convert_fusion.2.refs_0_ = bf16[2,16,800,256]{3,2,1,0:T(8,128)(2,1)} fusion(f32[2,16,256,800]{2,3,1,0:T(8,128)} %param.31), kind=kLoop, calls=%fused_computation.101 | loop fusion | flops 6553600 | bytes 39321600 | tf_op jit(solution)/shard_map/convert_element_type | solution.py:863
  21.6 15.2 %bitcast_convert_fusion.1.refs_2_ = bf16[2,16,800,256]{3,2,1,0:T(8,128)(2,1)} fusion(f32[2,16,256,800]{2,3,1,0:T(8,128)} %param.32), kind=kLoop, calls=%fused_computation.100 | loop fusion | flops 6553600 | bytes 39321600 | tf_op jit(solution)/shard_map/convert_element_type | solution.py:863
  36.8 16.5 %convert_element_type.132.refs_4_ = bf16[2,16,400,512]{3,2,1,0:T(8,128)(2,1)} convert(f32[2,16,400,512]{3,2,1,0:T(8,128)} %refs_8_.3) | non-fusion elementwise | flops 6553600 | bytes 39321600 | tf_op jit(solution)/shard_map/convert_element_type | solution.py:863
  56.6 6.7 bitcast_convert_fusion.wa_ref
  70.9 16.0 %all-gather.17.cloned.1.call-done = f32[8,320,128]{2,1,0:T(8,128)} async-done(((f32[1,320,128]{2,1,0:T(8,128)}), f32[8,320,128]{2,1,0:T(8,128)}) %all-gather.17.cloned.1.call-update) | async-done | bytes 1310736 | tf_op jit(solution)/shard_map/all_gather | solution.py:846
  86.9 2.1 copy.95
  90.1 16.1 %gather_fusion = bf16[1024,512]{1,0:T(8,128)(2,1)S(1)} fusion(f32[16032,512]{1,0:T(8,128)} %m_ref.1, s32[1024]{0:T(1024)S(1)} %broadcast_clamp_fusion), kind=kCustom, calls=%fused_computation | custom fusion | bytes 2101248 | tf_op jit(solution)/shard_map/jit(_take)/gather | solution.py:871
  111.2 2.1 copy-done.20
  113.3 4.2 attn_fwd.2.x_ref
  117.6 30.0 %moe_fwd.2 = (f32[512,512]{1,0:T(8,128)S(1)}, bf16[1280,512]{1,0:T(8,128)(2,1)}, f32[512,512]{1,0:T(8,128)S(1)}, f32[512,512]{1,0:T(8,128)S(1)}) custom-call(s32[17]{0:T(128)S(1)} %select_reduce_fusion.3.off, s32[2]{0:T(128)S(1)} %pad_add_fusion.1.fs, f32[512,512]{1,0:T(8,128)S(1)} %attn_fwd.2.x_ref, f32[1,512]{1,0:T(1,128)S(1)} %get-tuple-element.107.gain_ref, ...), custom_call_target="tpu_custom_call" | custom-call | flops 30000001024 | bytes 45000000 | tf_op jit(solution)/shard_map/moe_fwd/pallas_call | solution.py:322
  147.7 4.2 attn_fwd.3.x_ref
  152.0 29.4 %moe_fwd.3 = (f32[512,512]{1,0:T(8,128)S(1)}, bf16[1280,512]{1,0:T(8,128)(2,1)}, f32[512,512]{1,0:T(8,128)S(1)}, f32[512,512]{1,0:T(8,128)S(1)}) custom-call(s32[17]{0:T(128)S(1)} %select_reduce_fusion.2.off, s32[2]{0:T(128)S(1)} %pad_add_fusion.1.fs, f32[512,512]{1,0:T(8,128)S(1)} %attn_fwd.3.x_ref, f32[1,512]{1,0:T(1,128)S(1)} %get-tuple-element.105.gain_ref, ...), custom_call_target="tpu_custom_call" | custom-call | flops 30000001024 | bytes 45000000 | tf_op jit(solution)/shard_map/moe_fwd/pallas_call | solution.py:322
  183.3 78.8 %head_own.1 = (bf16[512,512]{1,0:T(8,128)(2,1)}, f32[72,512]{1,0:T(8,128)}, f32[512,512]{1,0:T(8,128)}, f32[1,512]{1,0:T(1,128)}, f32[1,512]{1,0:T(1,128)}) custom-call(s32[2]{0:T(128)} %copy-done.15, f32[512,512]{1,0:T(8,128)} %copy-done.29, f32[1,512]{1,0:T(1,128)} %get-tuple-element.104.gain_ref, s32[1,512]{1,0:T(1,128)} %lab_ref.1, ...), custom_call_target="tpu_custom_call" | custom-call | flops 54999998464 | bytes 70000000 | tf_op jit(solution)/shard_map/head_own/pallas_call | solution.py:534
  262.1 37.1 %moe_bwd.2 = (f32[512,512]{1,0:T(8,128)}, f32[1280,512]{1,0:T(8,128)}, f32[16,512]{1,0:T(8,128)}, f32[1,512]{1,0:T(1,128)}) custom-call(s32[17]{0:T(128)} %copy-done.18, s32[2]{0:T(128)} %copy-done.15, f32[512,512]{1,0:T(8,128)} %get-tuple-element.54.dx_ref, f32[512,512]{1,0:T(8,128)} %copy-done.24, f32[1,512]{1,0:T(1,128)} %copy-done.14, ...), custom_call_target="tpu_custom_call" | custom-call | flops 49999998976 | bytes 50000000 | tf_op jit(solution)/shard_map/moe_bwd/pallas_call | solution.py:344
  299.3 10.7 %attn_bwd.2 = (f32[512,512]{1,0:T(8,128)}, f32[2,264,1280]{2,1,0:T(8,128)}) custom-call(f32[512,512]{1,0:T(8,128)} %get-tuple-element.58.dx_ref, f32[512,512]{1,0:T(8,128)} %copy-done.23, f32[1,512]{1,0:T(1,128)} %copy-done.13, f32[512,128]{1,0:T(8,128)} %copy-done.6, f32[512,128]{1,0:T(8,128)} %copy-done.4, f32[16,512]{1,0:T(8,128)} %get-tuple-element.59.dwr_ref, ...), custom_call_target="tpu_custom_call" | custom-call | flops 15000000512 | bytes 10000000 | tf_op jit(solution)/shard_map/attn_bwd/pallas_call | solution.py:782
  309.9 37.2 %moe_bwd.3 = (f32[512,512]{1,0:T(8,128)}, f32[1280,512]{1,0:T(8,128)}, f32[16,512]{1,0:T(8,128)}, f32[1,512]{1,0:T(1,128)}) custom-call(s32[17]{0:T(128)} %copy-done.17, s32[2]{0:T(128)} %copy-done.15, f32[512,512]{1,0:T(8,128)} %get-tuple-element.63.dx_ref, f32[512,512]{1,0:T(8,128)} %copy-done.22, f32[1,512]{1,0:T(1,128)} %copy-done.12, ...), custom_call_target="tpu_custom_call" | custom-call | flops 49999998976 | bytes 50000000 | tf_op jit(solution)/shard_map/moe_bwd/pallas_call | solution.py:344
  347.2 10.7 %attn_bwd.3 = (f32[512,512]{1,0:T(8,128)}, f32[2,264,1280]{2,1,0:T(8,128)}) custom-call(f32[512,512]{1,0:T(8,128)} %get-tuple-element.67.dx_ref, f32[512,512]{1,0:T(8,128)} %copy-done.2, f32[1,512]{1,0:T(1,128)} %copy-done.11, f32[512,128]{1,0:T(8,128)} %copy-done.6, f32[512,128]{1,0:T(8,128)} %copy-done.4, f32[16,512]{1,0:T(8,128)} %get-tuple-element.68.dwr_ref, ...), custom_call_target="tpu_custom_call" | custom-call | flops 15000000512 | bytes 10000000 | tf_op jit(solution)/shard_map/attn_bwd/pallas_call | solution.py:782
  360.6 5.3 reduce-scatter.3.cloned.1.call-done
  365.9 11.8 %reduce-scatter.5.cloned.1.call-done = f32[1,264,1280]{2,1,0:T(8,128)} async-done(((f32[2,264,1280]{2,1,0:T(8,128)}), f32[1,264,1280]{2,1,0:T(8,128)}) %reduce-scatter.5.cloned.1.call-update) | async-done | bytes 1351696 | tf_op jit(solution)/shard_map/reduce_scatter | solution.py:900
  381.6 30.1 %all-gather.31.cloned.1.call-done = bf16[4096,512]{1,0:T(8,128)(2,1)} async-done(((bf16[512,512]{1,0:T(8,128)(2,1)}), bf16[4096,512]{1,0:T(8,128)(2,1)}) %all-gather.31.cloned.1.call-update) | async-done | bytes 4194320 | tf_op jit(solution)/shard_map/all_gather | solution.py:889
  411.7 20.1 %all-gather.33.cloned.1.call-done = f32[576,512]{1,0:T(8,128)} async-done(((f32[72,512]{1,0:T(8,128)}), f32[576,512]{1,0:T(8,128)}) %all-gather.33.cloned.1.call-update) | async-done | bytes 1179664 | tf_op jit(solution)/shard_map/all_gather | solution.py:890
  431.8 164.0 %head_dw.1 = (f32[32064,256]{1,0:T(8,128)}, f32[16032,256]{1,0:T(8,128)}) custom-call(s32[2]{0:T(128)} %copy-done.15, f32[1,1]{1,0:T(1,128)} %bitcast.105.lr_ref, bf16[8,512,512]{2,1,0:T(8,128)(2,1)} %bitcast.153, f32[8,72,512]{2,1,0:T(8,128)} %bitcast.154, s32[8,1,512]{2,1,0:T(1,128)} %broadcast_in_dim.65.lab_ref, ...), custom_call_target="tpu_custom_call" | custom-call | flops 140000002048 | bytes 70000000 | tf_op jit(solution)/shard_map/head_dw/pallas_call | solution.py:594
  596.1 5.2 sort.15
  602.1 2.8 copy-done.19
  604.9 38.8 %embed_upd.1 = f32[16032,512]{1,0:T(8,128)} custom-call(s32[13]{0:T(128)S(1)} %convert_reduce_fusion.bounds, s32[4096]{0:T(1024)S(1)} %get-tuple-element.50.keys, s32[4096]{0:T(1024)S(1)} %get-tuple-element.51.perm, f32[1,1]{1,0:T(1,128)} %bitcast.102.lr_ref, bf16[4096,512]{1,0:T(8,128)(2,1)S(1)} %copy-done.19, f32[16032,512]{1,0:T(8,128)} %m_ref.1), custom_call_target="tpu_custom_call" | custom-call | flops 24999999488 | bytes 66000000 | tf_op jit(solution)/shard_map/embed_upd/pallas_call | solution.py:659
  654.6 1.9 fusion.3
  658.0 1.8 fusion
  659.8 17.4 %head_upd.1 = f32[32064,256]{1,0:T(8,128)} custom-call(s32[2]{0:T(128)S(1)} %copy-done.16, f32[1,1]{1,0:T(1,128)} %bitcast.106.lr_ref, f32[16032,256]{1,0:T(8,128)} %collective-permute-done.5.grad_ref, f32[32064,256]{1,0:T(8,128)} %bitcast.118, f32[32064,256]{1,0:T(8,128)} %get-tuple-element.85.prev_ref), custom_call_target="tpu_custom_call", output_to_operand_aliasing={{}: (4, {})} | custom-call | flops 15000000512 | bytes 50000000 | tf_op jit(solution)/shard_map/head_upd/pallas_call | solution.py:623
  677.2 24.5 %all-gather.29.cloned.1.call-done = f32[10240,512]{1,0:T(8,128)} async-done(((f32[1280,512]{1,0:T(8,128)}), f32[10240,512]{1,0:T(8,128)}) %all-gather.29.cloned.1.call-update) | async-done | bytes 20971536 | tf_op jit(solution)/shard_map/all_gather | solution.py:898
  701.8 73.2 %expert_dw.2 = (f32[2,16,800,256]{3,2,1,0:T(8,128)}, f32[2,16,800,256]{3,2,1,0:T(8,128)}, f32[2,16,400,512]{3,2,1,0:T(8,128)}) custom-call(s32[8,17]{1,0:T(8,128)} %bitcast.148, s32[2]{0:T(128)} %copy-done.15, f32[1,1]{1,0:T(1,128)} %bitcast.103.lr_ref, bf16[8,1280,512]{2,1,0:T(8,128)(2,1)} %bitcast.152, f32[8,1280,512]{2,1,0:T(8,128)} %bitcast.151, ...), custom_call_target="tpu_custom_call" | custom-call | flops 60000002048 | bytes 150000000 | tf_op jit(solution)/shard_map/expert_dw/pallas_call | solution.py:437
  775.0 89.8 %all-gather.25.cloned.1.call-done = f32[10240,512]{1,0:T(8,128)} async-done(((f32[1280,512]{1,0:T(8,128)}), f32[10240,512]{1,0:T(8,128)}) %all-gather.25.cloned.1.call-update) | async-done | bytes 20971536 | tf_op jit(solution)/shard_map/all_gather | solution.py:898
  864.8 73.6 %expert_dw.3 = (f32[2,16,800,256]{3,2,1,0:T(8,128)}, f32[2,16,800,256]{3,2,1,0:T(8,128)}, f32[2,16,400,512]{3,2,1,0:T(8,128)}) custom-call(s32[8,17]{1,0:T(8,128)} %bitcast.140, s32[2]{0:T(128)} %copy-done.15, f32[1,1]{1,0:T(1,128)} %bitcast.104.lr_ref, ...), custom_call_target="tpu_custom_call", output_to_operand_aliasing={{0}: (14, {}), {1}: (15, {}), {2}: (16, {})} | custom-call | flops 60000002048 | bytes 150000000 | tf_op jit(solution)/shard_map/expert_dw/pallas_call | solution.py:437
  (261 shorter events, 38.6 us)
Async XLA Ops:
  7.2 79.7 %all-gather.17.cloned.1.call-start = ((), (), s32[]{:S(2)}) async-start(), calls=%async_computation.2 | async-start | bytes 1474560 | tf_op jit(solution)/shard_map/all_gather | solution.py:846
  20.7 96.7 %collective-permute-start.1 = (bf16[2,16,800,256]{3,2,1,0:T(8,128)(2,1)}, bf16[2,16,800,256]{3,2,1,0:T(8,128)(2,1)}, u32[]{:S(2)}, u32[]{:S(2)}) collective-permute-start(bf16[2,16,800,256]{3,2,1,0:T(8,128)(2,1)} %bitcast_convert_fusion.2.refs_0_), channel_id=1, source_target_pairs={{0,1},{1,0},{2,3},{3,2},{4,5},{5,4},{6,7},{7,6}} | collective-permute-start | bytes 39321608 | tf_op jit(solution)/shard_map/ppermute | solution.py:864
  36.8 80.7 %collective-permute-start.2 = (bf16[2,16,800,256]{3,2,1,0:T(8,128)(2,1)}, bf16[2,16,800,256]{3,2,1,0:T(8,128)(2,1)}, u32[]{:S(2)}, u32[]{:S(2)}) collective-permute-start(bf16[2,16,800,256]{3,2,1,0:T(8,128)(2,1)} %bitcast_convert_fusion.1.refs_2_), channel_id=1, source_target_pairs={{0,1},{1,0},{2,3},{3,2},{4,5},{5,4},{6,7},{7,6}} | collective-permute-start | bytes 39321608 | tf_op jit(solution)/shard_map/ppermute | solution.py:864
  53.5 64.0 %collective-permute-start.3 = (bf16[2,16,400,512]{3,2,1,0:T(8,128)(2,1)}, bf16[2,16,400,512]{3,2,1,0:T(8,128)(2,1)}, u32[]{:S(2)}, u32[]{:S(2)}) collective-permute-start(bf16[2,16,400,512]{3,2,1,0:T(8,128)(2,1)} %convert_element_type.132.refs_4_), channel_id=1, source_target_pairs={{0,1},{1,0},{2,3},{3,2},{4,5},{5,4},{6,7},{7,6}} | collective-permute-start | bytes 39321608 | tf_op jit(solution)/shard_map/ppermute | solution.py:864
  63.3 120.1 %collective-permute-start.4 = (bf16[32064,256]{1,0:T(8,128)(2,1)}, bf16[32064,256]{1,0:T(8,128)(2,1)}, u32[]{:S(2)}, u32[]{:S(2)}) collective-permute-start(bf16[32064,256]{1,0:T(8,128)(2,1)} %bitcast_convert_fusion.wa_ref), channel_id=1, source_target_pairs={{0,1},{1,0},{2,3},{3,2},{4,5},{5,4},{6,7},{7,6}} | collective-permute-start | bytes 49250312 | tf_op jit(solution)/shard_map/ppermute | solution.py:864
  63.5 54.0 %copy-start = (s32[1,1,512,2]{3,2,1,0:T(8,128)}, s32[1,1,512,2]{3,2,1,0:T(8,128)S(1)}, u32[]{:S(2)}) copy-start(s32[1,1,512,2]{3,2,1,0:T(8,128)S(1)} %copy.88) | copy-start | bytes 12292
  63.7 88.1 %copy-start.1 = (s32[1,1,512,2]{3,2,1,0:T(8,128)}, s32[1,1,512,2]{3,2,1,0:T(8,128)S(1)}, u32[]{:S(2)}) copy-start(s32[1,1,512,2]{3,2,1,0:T(8,128)S(1)} %copy.89) | copy-start | bytes 12292
  64.1 53.4 %copy-start.17 = (s32[17]{0:T(128)}, s32[17]{0:T(128)S(1)}, u32[]{:S(2)}) copy-start(s32[17]{0:T(128)S(1)} %select_reduce_fusion.3.off) | copy-start | bytes 208
  64.4 87.5 %copy-start.18 = (s32[17]{0:T(128)}, s32[17]{0:T(128)S(1)}, u32[]{:S(2)}) copy-start(s32[17]{0:T(128)S(1)} %select_reduce_fusion.2.off) | copy-start | bytes 208
  65.3 45.8 %all-gather.19.cloned.1.call-start = ((), (), s32[]{:S(2)}) async-start(), calls=%async_computation.3 | async-start | bytes 3932160 | tf_op jit(solution)/shard_map/all_gather | solution.py:860
  66.8 299.1 %reduce-scatter.3.cloned.1.call-start = ((), (), s32[]{:S(2)}) async-start(), calls=%async_computation.4 | async-start | bytes 4055040 | tf_op jit(solution)/shard_map/reduce_scatter | solution.py:900
  67.4 50.1 %copy-start.3 = (s32[512,2]{1,0:T(8,128)}, s32[512,2]{1,0:T(8,128)S(1)}, u32[]{:S(2)}) copy-start(s32[512,2]{1,0:T(8,128)S(1)} %get-tuple-element.102.pcol_ref) | copy-start | bytes 12292
  67.5 50.0 %copy-start.9 = (s32[2,512]{1,0:T(2,128)}, s32[2,512]{1,0:T(2,128)S(1)}, u32[]{:S(2)}) copy-start(s32[2,512]{1,0:T(2,128)S(1)} %copy.79.prow_ref) | copy-start | bytes 12292
  68.0 83.9 %copy-start.5 = (s32[512,2]{1,0:T(8,128)}, s32[512,2]{1,0:T(8,128)S(1)}, u32[]{:S(2)}) copy-start(s32[512,2]{1,0:T(8,128)S(1)} %get-tuple-element.100.pcol_ref) | copy-start | bytes 12292
  68.1 83.8 %copy-start.10 = (s32[2,512]{1,0:T(2,128)}, s32[2,512]{1,0:T(2,128)S(1)}, u32[]{:S(2)}) copy-start(s32[2,512]{1,0:T(2,128)S(1)} %copy.81.prow_ref) | copy-start | bytes 12292
  69.6 82.3 %copy-start.15 = (s32[2]{0:T(128)}, s32[2]{0:T(128)S(1)}, u32[]{:S(2)}) copy-start(s32[2]{0:T(128)S(1)} %pad_add_fusion.1.fs) | copy-start | bytes 28
  70.8 76.9 %copy-start.6 = (f32[512,128]{1,0:T(8,128)}, f32[512,128]{1,0:T(8,128)S(1)}, u32[]{:S(2)}) copy-start(f32[512,128]{1,0:T(8,128)S(1)} %pad_maximum_fusion.1.cos_ref) | copy-start | bytes 786436
  70.9 76.7 %copy-start.4 = (f32[512,128]{1,0:T(8,128)}, f32[512,128]{1,0:T(8,128)S(1)}, u32[]{:S(2)}) copy-start(f32[512,128]{1,0:T(8,128)S(1)} %pad_maximum_fusion.2.sin_ref) | copy-start | bytes 786436
  107.6 2.3 collective-permute-start
  183.3 78.8 %copy-start.28 = (f32[512,512]{1,0:T(8,128)}, f32[512,512]{1,0:T(8,128)S(1)}, u32[]{:S(2)}) copy-start(f32[512,512]{1,0:T(8,128)S(1)} %get-tuple-element.56.y1_ref) | copy-start | bytes 3145732
  357.9 19.8 %reduce-scatter.5.cloned.1.call-start = ((), (), s32[]{:S(2)}) async-start(), calls=%async_computation.5 | async-start | bytes 4055040 | tf_op jit(solution)/shard_map/reduce_scatter | solution.py:900
  358.5 53.3 %all-gather.31.cloned.1.call-start = ((), (), s32[]{:S(2)}) async-start(), calls=%async_computation.11 | async-start | bytes 4718592 | tf_op jit(solution)/shard_map/all_gather | solution.py:889
  359.0 72.7 %all-gather.33.cloned.1.call-start = ((), (), s32[]{:S(2)}) async-start(), calls=%async_computation.12 | async-start | bytes 1327104 | tf_op jit(solution)/shard_map/all_gather | solution.py:890
  359.6 242.5 %all-gather.21.cloned.1.call-start = ((), (), s32[]{:S(2)}) async-start(), calls=%async_computation.6 | async-start | bytes 4718592 | tf_op jit(solution)/shard_map/all_gather | solution.py:902
  360.6 283.2 %all-reduce.4.cloned.1.call-start = ((), (), s32[]{:S(2)}) async-start(), calls=%async_computation.13 | async-start | bytes 5406720 | tf_op jit(solution)/shard_map/psum | solution.py:900
  377.7 299.6 %all-gather.27.cloned.1.call-start = ((), (), s32[]{:S(2)}) async-start(), calls=%async_computation.9 | async-start | bytes 11796480 | tf_op jit(solution)/shard_map/all_gather | solution.py:885
  378.4 323.4 %all-gather.29.cloned.1.call-start = ((), (), s32[]{:S(2)}) async-start(), calls=%async_computation.10 | async-start | bytes 23592960 | tf_op jit(solution)/shard_map/all_gather | solution.py:898
  379.0 396.0 %all-gather.23.cloned.1.call-start = ((), (), s32[]{:S(2)}) async-start(), calls=%async_computation.7 | async-start | bytes 11796480 | tf_op jit(solution)/shard_map/all_gather | solution.py:885
  379.7 485.1 %all-gather.25.cloned.1.call-start = ((), (), s32[]{:S(2)}) async-start(), calls=%async_computation.8 | async-start | bytes 23592960 | tf_op jit(solution)/shard_map/all_gather | solution.py:898
  431.8 164.2 %slice-start.8 = ((s32[8,1058]{1,0:T(8,128)}), s32[8,34]{1,0:T(8,128)S(1)}, s32[]{:S(2)}) async-start(s32[8,1058]{1,0:T(8,128)} %copy-done.40), calls=%async_computation.22 | async-start | bytes 8192 | tf_op jit(solution)/shard_map/slice | solution.py:857
  431.8 164.3 %copy-start.43 = (s32[1,4,8,128]{3,2,1,0:T(8,128)S(1)}, s32[1,4,8,128]{3,2,1,0:T(8,128)}, u32[]{:S(2)}) copy-start(s32[1,4,8,128]{3,2,1,0:T(8,128)} %get-tuple-element.118) | copy-start | bytes 49156
  595.7 64.0 %collective-permute-start.5 = (f32[16032,256]{1,0:T(8,128)}, f32[16032,256]{1,0:T(8,128)}, u32[]{:S(2)}, u32[]{:S(2)}) collective-permute-start(f32[16032,256]{1,0:T(8,128)} %get-tuple-element.84), channel_id=1, source_target_pairs={{0,1},{1,0},{2,3},{3,2},{4,5},{5,4},{6,7},{7,6}} | collective-permute-start | bytes 49250312 | tf_op jit(solution)/shard_map/ppermute | solution.py:906
  (50 other events, 815.6 us)
Sparse Core Ops, SparseCore 0:
  65.4 21.4 all-gather.16
  89.0 10.2 all-gather.18
  358.0 7.8 reduce-scatter.2
  368.5 9.0 reduce-scatter.4
  379.3 32.3 all-gather.30
  413.4 18.3 all-gather.32
  434.2 31.0 all-gather.20
  468.5 68.7 all-reduce.3
  539.2 57.7 all-gather.26
  598.6 103.1 all-gather.28
  703.6 57.5 all-gather.22
  762.9 101.8 all-gather.24

commit v2 on v1

--- a/solution.py
+++ b/solution.py
@@ -16,7 +16,7 @@
 I32 = jnp.int32
 TILE = 16
 HEAD_STEPS = 12
-HEAD_PIECE = 512
+HEAD_PIECE = 256
 DW_PIECE = 384
 LSE_ROWS = 72
 KNOWN = 40960
@@ -359,11 +359,11 @@
 
 def expert_dw_kernel(off, fs, lr_ref, xs_hbm, dys_hbm, *refs, blk, alias):
     w_refs, masters, refs = refs[:6], refs[6:9], refs[12 if alias else 9 :]
-    outs, (xbuf, dbuf, sems), accs = refs[:3], refs[3:6], refs[6:]
-    acc_g, acc_u, acc_d = accs
+    outs, (xbuf, dbuf, sems) = refs[:3], refs[3:]
     expert = pl.program_id(0)
     seqs = xs_hbm.shape[0]
-    half = acc_g.shape[COL]
+    half = outs[0].shape[-1]
+    lr = get(lr_ref)
     mine = fs[0]
     weights = ExpertWeights(w_refs, mine)
 
@@ -395,10 +395,8 @@
     total = pl.multiple_of(copies(expert, slot, lambda copy: copy.wait()), TILE)
     for buf in (xbuf, dbuf):
         buf[slot, pl.ds(total, blk)] = jnp.zeros((blk, buf.shape[2]), buf.dtype)
-    for acc in accs:
-        fill(acc, 0)
-
-    def body(i, carry):
+
+    def block(i, bases):
         rows = pl.ds(pl.multiple_of(i * blk, blk), blk)
         xs = own_first(xbuf[slot, rows], mine)
         dys = dbuf[slot, rows].astype(BF16)
@@ -407,20 +405,26 @@
         def gradients(core):
             return glu_bwd(dot(weights.gate(core), xs_t), dot(weights.up(core), xs_t), dot(weights.down(core), dys_t))
 
+        def take(which, part, grad):
+            outs[which][0, 0, part] = bases[which][0, 0, part] - lr * grad
+
         def add(core, made):
             d_gate, d_up, hidden = made
             part = weights.rows_of(core)
-            acc_g[part] += dot(d_gate, own)
-            acc_u[part] += dot(d_up, own)
+            take(0, part, dot(d_gate, own))
+            take(1, part, dot(d_up, own))
             if core is weights.cores[0]:
-                put(acc_d, get(acc_d) + dot(hidden, dys))
+                take(2, slice(None), dot(hidden, dys))
 
         staggered(weights.cores, gradients, add)
+
+    block(0, masters)
+
+    def more(i, carry):
+        block(i, outs)
         return carry
 
-    lax.fori_loop(0, (total + blk - 1) // blk, body, 0)
-    for out, master, acc in zip(outs, masters, accs):
-        put(out, get(master) - get(lr_ref) * get(acc).reshape(out.shape))
+    lax.fori_loop(1, (total + blk - 1) // blk, more, 0)
 
 
 def expert_dw(layer, off, fs, lr, xs, dys, weights, masters, prev):
@@ -446,8 +450,7 @@
                 pltpu.VMEM((2, most, width), BF16),
                 pltpu.VMEM((2, most, width), F32),
                 pltpu.SemaphoreType.DMA((2, 2)),
-            ]
-            + [pltpu.VMEM(m.shape[2:], F32) for m in masters],
+            ],
         ),
         input_output_aliases={first_prev + k: k for k in range(3)} if alias else {},
         compiler_params=params(62),
@@ -674,6 +677,51 @@
         cost_estimate=cost(25, 66),
         name="embed_upd",
     )(bounds, keys, perm, lr, grads, master)
+
+
+def small_upd_kernel(lr_ref, *refs, layers):
+    reduced, refs = refs[:layers], refs[layers:]
+    masters, outs, loss_out = refs[: len(refs) // 2], refs[len(refs) // 2 : -1], refs[-1]
+    lr = get(lr_ref)
+    for l, grads in enumerate(reduced):
+        half = masters[0].shape[1]
+        wide = grads.shape[COL]
+        at = 0
+        for master, out in list(zip(masters, outs))[:4]:
+            count = master.shape[2]
+            out[l] = master[l] - lr * grads[:half, at : at + count]
+            at += count
+
+        def small(i):
+            return grads[half + i * half // wide : half + i * half // wide + 1, i * half % wide : i * half % wide + half]
+
+        router, gain_attn, gain_mlp, gain_final = list(zip(masters, outs))[4:]
+        experts = router[0].shape[1]
+        for i in range(experts):
+            row = slice(i, i + 1)
+            router[1][l, row] = router[0][l, row] - lr * small(i)
+        own = slice(l, l + 1)
+        for i, (master, out) in enumerate((gain_attn, gain_mlp)):
+            out[own] = master[own] - lr * small(experts + i)
+        if l == 0:
+            put(gain_final[1], get(gain_final[0]) - lr * small(experts + 2))
+            put(loss_out, small(experts + 3))
+
+
+def small_upd(lr, reduced, masters):
+    half = masters[0].shape[1]
+    args = [lr, *reduced, *masters]
+    out_shapes = [jax.ShapeDtypeStruct(m.shape, F32) for m in masters] + [jax.ShapeDtypeStruct((1, half), F32)]
+    return pl.pallas_call(
+        functools.partial(small_upd_kernel, layers=len(reduced)),
+        out_shape=out_shapes,
+        grid=(1,),
+        in_specs=[whole(a.shape) for a in args],
+        out_specs=[whole(o.shape) for o in out_shapes],
+        compiler_params=params(48),
+        cost_estimate=cost(4, 10),
+        name="small_upd",
+    )(*args)
 
 
 def rope_tables(positions):
@@ -805,6 +853,10 @@
     return jnp.sum(hot * place[:, None, :], axis=2).astype(I32), starts
 
 
+def after(x, earlier):
+    return lax.optimization_barrier((x, earlier))[0]
+
+
 def solution(mesh):
     device_count = mesh.shape['rep'] * mesh.shape['fsdp']
     both = ('rep', 'fsdp')
@@ -833,12 +885,13 @@
         m_gate = jnp.swapaxes(w_gate, 2, 3)
         m_up = jnp.swapaxes(w_up, 2, 3)
         m_head = w_head.T
+        router_t = jnp.swapaxes(w_router, 1, 2)
 
         experts_of = expert_idx[:, 0]
         placed = [routing(experts_of[l], experts) for l in range(layers)]
         starts = jnp.stack([s for _, s in placed])
         ints = jnp.concatenate([tok_ids[0], tok_labels[0], starts.reshape(-1)]).astype(F32)
-        misc = jnp.concatenate([jnp.swapaxes(w_router, 1, 2).reshape(layers * experts, half), g_attn, g_mlp, g_final[None]])
+        misc = jnp.concatenate([router_t.reshape(layers * experts, half), g_attn, g_mlp, g_final[None]])
         misc = misc.astype(BF16).astype(F32).reshape(-1)
         packed = jnp.concatenate([misc, ints])
         n_misc = misc.shape[0]
@@ -863,13 +916,13 @@
             rounded = x.astype(BF16)
             return rounded, lax.ppermute(rounded, 'fsdp', swap)
 
-        expert_w = with_partner(m_gate) + with_partner(m_up) + with_partner(w_down)
-        head_w = with_partner(m_head)
+        expert_w = with_partner(after(m_gate, packed)) + with_partner(after(m_up, packed)) + with_partner(after(w_down, packed))
 
         partner_ids = lax.dynamic_index_in_dim(ids_all, pair * 2 + 1 - me, 0, keepdims=False)
         wanted = jnp.concatenate([tok_ids[0], partner_ids]) - me * vocab_share
         taken = jnp.take(embedding, jnp.clip(wanted, 0, vocab_share - 1), axis=0).astype(BF16)
         sent = lax.ppermute(taken[toks:], 'fsdp', swap)
+        head_w = with_partner(after(m_head, taken))
         is_mine = (wanted[:toks] >= 0) & (wanted[:toks] < vocab_share)
         x = jnp.where(is_mine[:, None], taken[:toks], sent).astype(F32)
 
@@ -901,14 +954,17 @@
 
         d_rows = lax.all_gather(dx.astype(BF16), both).reshape(tokens_all, width)
 
-        fin_all, _ = lax.optimization_barrier((fin_all, dx))
+        fin_all = after(fin_all, dx)
         new_head, other_grad = head_dw(fs, lr, fin_all, lse_all, labels_all[:, None], *head_w, m_head, tokens_all)
         other_grad = lax.ppermute(other_grad, 'fsdp', swap)
+        dys_all[1] = after(dys_all[1], new_head)
         new_experts = None
         for l in reversed(range(layers)):
             new_experts = expert_dw(l, starts_all[:, l], fs, lr, xs_all[l], dys_all[l], expert_w, (m_gate, m_up, w_down), new_experts)
 
-        new_head = head_upd(fs, lr, other_grad, m_head, new_head)
+        small_masters = (w_query, w_key, w_value, w_attn_out, router_t, g_attn, g_mlp, g_final[None])
+        *small_new, total_loss = small_upd(lr, reduced, small_masters)
+        new_head = head_upd(fs, lr, after(other_grad, new_experts[0]), m_head, new_head)
 
         block = 1336
         local_id = ids_all.reshape(-1) - me * vocab_share
@@ -916,26 +972,11 @@
         keys, perm = lax.sort((key, lax.iota(I32, tokens_all)), num_keys=1)
         edges = jnp.arange(vocab_share // block + 1, dtype=I32) * block
         bounds = jnp.sum(key[None, :] < edges[:, None], axis=1).astype(I32)
-        new_embedding = embed_upd(bounds, keys, perm, lr, d_rows, embedding, block)
-
-        def update(master, pick):
-            return master - learn_rate * jnp.stack([pick(reduced[l]) for l in range(layers)])
-
-        def tail_of(r, first, count):
-            return r[half:].reshape(-1)[first * half : (first + count) * half].reshape(count, half)
-
-        v_at = q_width + kv_width
-        new_query = update(w_query, lambda r: r[:half, :q_width])
-        new_key = update(w_key, lambda r: r[:half, q_width:v_at])
-        new_value = update(w_value, lambda r: r[:half, v_at : v_at + kv_width])
-        new_attn_out = update(w_attn_out, lambda r: r[:half, v_at + kv_width :])
-        new_router = update(w_router, lambda r: tail_of(r, 0, experts).T)
-        new_g_attn = update(g_attn, lambda r: tail_of(r, experts, 1)[0])
-        new_g_mlp = update(g_mlp, lambda r: tail_of(r, experts + 1, 1)[0])
-        new_final = g_final - learn_rate * tail_of(reduced[0], experts + 2, 1)[0]
-        both_loss = tail_of(reduced[0], experts + 3, 1)[0, 0]
+        new_embedding = embed_upd(bounds, keys, perm, lr, after(d_rows, new_experts[0]), embedding, block)
+
+        new_query, new_key, new_value, new_attn_out, new_router, new_g_attn, new_g_mlp, new_final = small_new
         new_gate, new_up, new_down = new_experts
-        return (new_embedding, new_query, new_key, new_value, new_attn_out, new_g_attn, new_g_mlp, new_router,
-                jnp.swapaxes(new_gate, 2, 3), jnp.swapaxes(new_up, 2, 3), new_down, new_final, new_head.T, both_loss)
+        return (new_embedding, new_query, new_key, new_value, new_attn_out, new_g_attn, new_g_mlp, jnp.swapaxes(new_router, 1, 2),
+                jnp.swapaxes(new_gate, 2, 3), jnp.swapaxes(new_up, 2, 3), new_down, new_final[0], new_head.T, total_loss[0, 0])
 
     return jax.shard_map(step, mesh=mesh, in_specs=in_specs, out_specs=out_specs, check_vma=False)

time: 952 us -> 957 us (level)
  waiting for transfers between devices: 202 us -> 229 us
  Pallas kernels: 609 us -> 591 us
    all_gather x2, waiting for transfers between devices: 0.02 us -> 58.9 us  [step(): xs_all.append(lax.all_gather(xs, both))]
    all_gather x1, waiting for transfers between devices: 30.1 us -> 10.9 us  [step(): fin_all = lax.all_gather(fin, both)]
    ppermute x1, waiting for transfers between devices: 0.01 us -> 18.6 us  [step(): sent = lax.ppermute(taken[toks:], 'fsdp', swap)]
    all_gather x2, waiting for transfers between devices: 114 us -> 96.5 us  [step(): dys_all[l] = lax.all_gather(dys, both)]
    all_gather x1, waiting for transfers between devices: 16 us -> 0.01 us  [step(): known = lax.all_gather(packed, both).reshape(device_count, -1)]
    pallas_call x2, Pallas kernels: 147 us -> 134 us  [expert_dw(): pl.pallas_call(functools.partial(expert_dw_kernel, blk=blk, alias=alias),...]
  transfers between devices with their start and end apart: 18 -> 18, of which waited for: 7 -> 7; matrix products, arithmetic and copies ran while one was open for 10% -> 9% of each run, Pallas kernels for 38% -> 39%
where the time goes in v2:
time: 957 us; the launch traced here: 947 us
  Pallas kernels  591 us (62%)
  waiting for transfers between devices  229 us (24%)
  other arithmetic  68.1 us (7%)
  local copies, waits for them, and re-layouts  38.1 us (4%)
  between operations  17.4 us (2%)
    pallas_call x1, Pallas kernels, head_dw(): pl.pallas_call(functools.partial(head_dw_kernel, tokens_all=tokens_all),...  164 us
    pallas_call x2, Pallas kernels, expert_dw(): pl.pallas_call(functools.partial(expert_dw_kernel, blk=blk, alias=alias),...  134 us
    all_gather x2, waiting for transfers between devices, step(): dys_all[l] = lax.all_gather(dys, both)  96.5 us
    pallas_call x2, Pallas kernels, moe_bwd(): pl.pallas_call(functools.partial(moe_bwd_kernel, rows=rows, blk=blk), out...  74.2 us
    pallas_call x1, Pallas kernels, head(): pl.pallas_call(functools.partial(head_kernel, tokens_all=tokens_all), out...  72.2 us
    pallas_call x2, Pallas kernels, moe_fwd(): pl.pallas_call(functools.partial(moe_fwd_kernel, rows=rows, blk=blk), out...  59.5 us
    all_gather x2, waiting for transfers between devices, step(): xs_all.append(lax.all_gather(xs, both))  58.9 us
    convert_element_type x4, other arithmetic, with_partner(): rounded = x.astype(BF16)  50.9 us
  transfers between devices with their start and end apart: 18, of which 7 were waited for; matrix products, arithmetic and copies ran while one was open for 9% of the time, Pallas kernels for 39%

profile of v2, /device:TPU:0, one launch (start us, length us, event | category | flops | bytes accessed | tf_op | source)
XLA Modules:
  0.0 947.0 jit_solution(12764915017464581684)
XLA Ops:
  14.2 13.7 %convert_element_type.130.refs_0_ = bf16[2,16,800,256]{3,2,1,0:T(8,128)(2,1)} convert(f32[2,16,800,256]{3,2,1,0:T(8,128)} %bitcast.97) | non-fusion elementwise | flops 6553600 | bytes 39321600 | tf_op jit(solution)/shard_map/convert_element_type | solution.py:916
  28.8 6.5 copy-done.44
  35.3 5.6 convert_element_type.131.refs_2_
  41.8 13.6 %convert_element_type.132.refs_4_ = bf16[2,16,400,512]{3,2,1,0:T(8,128)(2,1)} convert(f32[2,16,400,512]{3,2,1,0:T(8,128)} %refs_8_.4) | non-fusion elementwise | flops 6553600 | bytes 39321600 | tf_op jit(solution)/shard_map/convert_element_type | solution.py:916
  55.3 2.1 copy.93
  58.5 14.3 %gather_fusion = bf16[1024,512]{1,0:T(8,128)(2,1)S(1)} fusion(f32[16032,512]{1,0:T(8,128)} %m_ref.1, s32[1024]{0:T(1024)S(1)} %broadcast_clamp_fusion), kind=kCustom, calls=%fused_computation | custom fusion | bytes 2101248 | tf_op jit(solution)/shard_map/jit(_take)/gather | solution.py:923
  73.3 18.0 %convert_element_type.138.wa_ref = bf16[32064,256]{1,0:T(8,128)(2,1)} convert(f32[32064,256]{1,0:T(8,128)} %bitcast.94) | non-fusion elementwise | flops 8208384 | bytes 49250304 | tf_op jit(solution)/shard_map/convert_element_type | solution.py:916
  100.2 18.6 %collective-permute-done = bf16[512,512]{1,0:T(8,128)(2,1)S(1)} collective-permute-done((bf16[512,512]{1,0:T(8,128)(2,1)}, bf16[512,512]{1,0:T(8,128)(2,1)S(1)}, u32[]{:S(2)}, u32[]{:S(2)}) %collective-permute-start) | collective-permute-done | bytes 524320 | tf_op jit(solution)/shard_map/ppermute | solution.py:924
  120.1 2.1 copy-done.32
  122.2 4.2 attn_fwd.2.x_ref
  126.5 29.9 %moe_fwd.2 = (f32[512,512]{1,0:T(8,128)S(1)}, bf16[1280,512]{1,0:T(8,128)(2,1)}, f32[512,512]{1,0:T(8,128)S(1)}, f32[512,512]{1,0:T(8,128)S(1)}) custom-call(s32[17]{0:T(128)S(1)} %select_reduce_fusion.3.off, s32[2]{0:T(128)S(1)} %pad_add_fusion.1.fs, f32[512,512]{1,0:T(8,128)S(1)} %attn_fwd.2.x_ref, f32[1,512]{1,0:T(1,128)S(1)} %get-tuple-element.131.gain_ref, ...), custom_call_target="tpu_custom_call" | custom-call | flops 30000001024 | bytes 45000000 | tf_op jit(solution)/shard_map/moe_fwd/pallas_call | solution.py:322
  156.4 4.2 attn_fwd.3.x_ref
  160.7 29.6 %moe_fwd.3 = (f32[512,512]{1,0:T(8,128)S(1)}, bf16[1280,512]{1,0:T(8,128)(2,1)}, f32[512,512]{1,0:T(8,128)S(1)}, f32[512,512]{1,0:T(8,128)S(1)}) custom-call(s32[17]{0:T(128)S(1)} %select_reduce_fusion.2.off, s32[2]{0:T(128)S(1)} %pad_add_fusion.1.fs, f32[512,512]{1,0:T(8,128)S(1)} %attn_fwd.3.x_ref, f32[1,512]{1,0:T(1,128)S(1)} %get-tuple-element.129.gain_ref, ...), custom_call_target="tpu_custom_call" | custom-call | flops 30000001024 | bytes 45000000 | tf_op jit(solution)/shard_map/moe_fwd/pallas_call | solution.py:322
  192.3 72.2 %head_own.1 = (bf16[512,512]{1,0:T(8,128)(2,1)}, f32[72,512]{1,0:T(8,128)}, f32[512,512]{1,0:T(8,128)}, f32[1,512]{1,0:T(1,128)}, f32[1,512]{1,0:T(1,128)}) custom-call(s32[2]{0:T(128)} %copy-done.26, f32[512,512]{1,0:T(8,128)} %copy-done.43, f32[1,512]{1,0:T(1,128)} %get-tuple-element.128.gain_ref, s32[1,512]{1,0:T(1,128)} %lab_ref.1, ...), custom_call_target="tpu_custom_call" | custom-call | flops 54999998464 | bytes 70000000 | tf_op jit(solution)/shard_map/head_own/pallas_call | solution.py:537
  264.5 37.0 %moe_bwd.2 = (f32[512,512]{1,0:T(8,128)}, f32[1280,512]{1,0:T(8,128)}, f32[16,512]{1,0:T(8,128)}, f32[1,512]{1,0:T(1,128)}) custom-call(s32[17]{0:T(128)} %copy-done.30, s32[2]{0:T(128)} %copy-done.26, f32[512,512]{1,0:T(8,128)} %get-tuple-element.74.dx_ref, f32[512,512]{1,0:T(8,128)} %copy-done.38, f32[1,512]{1,0:T(1,128)} %copy-done.23, ...), custom_call_target="tpu_custom_call" | custom-call | flops 49999998976 | bytes 50000000 | tf_op jit(solution)/shard_map/moe_bwd/pallas_call | solution.py:344
  301.6 10.7 %attn_bwd.2 = (f32[512,512]{1,0:T(8,128)}, f32[2,264,1280]{2,1,0:T(8,128)}) custom-call(f32[512,512]{1,0:T(8,128)} %get-tuple-element.78.dx_ref, f32[512,512]{1,0:T(8,128)} %copy-done.37, f32[1,512]{1,0:T(1,128)} %copy-done.22, f32[512,128]{1,0:T(8,128)} %copy-done.12, f32[512,128]{1,0:T(8,128)} %copy-done.13, f32[16,512]{1,0:T(8,128)} %get-tuple-element.79.dwr_ref, ...), custom_call_target="tpu_custom_call" | custom-call | flops 15000000512 | bytes 10000000 | tf_op jit(solution)/shard_map/attn_bwd/pallas_call | solution.py:830
  312.2 37.2 %moe_bwd.3 = (f32[512,512]{1,0:T(8,128)}, f32[1280,512]{1,0:T(8,128)}, f32[16,512]{1,0:T(8,128)}, f32[1,512]{1,0:T(1,128)}) custom-call(s32[17]{0:T(128)} %copy-done.29, s32[2]{0:T(128)} %copy-done.26, f32[512,512]{1,0:T(8,128)} %get-tuple-element.83.dx_ref, f32[512,512]{1,0:T(8,128)} %copy-done.36, f32[1,512]{1,0:T(1,128)} %copy-done.21, ...), custom_call_target="tpu_custom_call" | custom-call | flops 49999998976 | bytes 50000000 | tf_op jit(solution)/shard_map/moe_bwd/pallas_call | solution.py:344
  349.4 10.7 %attn_bwd.3 = (f32[512,512]{1,0:T(8,128)}, f32[2,264,1280]{2,1,0:T(8,128)}) custom-call(f32[512,512]{1,0:T(8,128)} %get-tuple-element.87.dx_ref, f32[512,512]{1,0:T(8,128)} %copy-done.6, f32[1,512]{1,0:T(1,128)} %copy-done.20, f32[512,128]{1,0:T(8,128)} %copy-done.12, f32[512,128]{1,0:T(8,128)} %copy-done.13, f32[16,512]{1,0:T(8,128)} %get-tuple-element.88.dwr_ref, ...), custom_call_target="tpu_custom_call" | custom-call | flops 15000000512 | bytes 10000000 | tf_op jit(solution)/shard_map/attn_bwd/pallas_call | solution.py:830
  362.2 7.8 reduce-scatter.3.cloned.1.call-done
  370.0 11.7 %reduce-scatter.5.cloned.1.call-done = f32[1,264,1280]{2,1,0:T(8,128)} async-done(((f32[2,264,1280]{2,1,0:T(8,128)}), f32[1,264,1280]{2,1,0:T(8,128)}) %reduce-scatter.5.cloned.1.call-update) | async-done | bytes 1351696 | tf_op jit(solution)/shard_map/reduce_scatter | solution.py:953
  385.7 10.9 %all-gather.31.cloned.1.call-done = bf16[4096,512]{1,0:T(8,128)(2,1)} async-done(((bf16[512,512]{1,0:T(8,128)(2,1)}), bf16[4096,512]{1,0:T(8,128)(2,1)}) %all-gather.31.cloned.1.call-update) | async-done | bytes 4194320 | tf_op jit(solution)/shard_map/all_gather | solution.py:942
  396.6 20.2 %all-gather.33.cloned.1.call-done = f32[576,512]{1,0:T(8,128)} async-done(((f32[72,512]{1,0:T(8,128)}), f32[576,512]{1,0:T(8,128)}) %all-gather.33.cloned.1.call-update) | async-done | bytes 1179664 | tf_op jit(solution)/shard_map/all_gather | solution.py:943
  416.8 164.0 %head_dw.1 = (f32[32064,256]{1,0:T(8,128)}, f32[16032,256]{1,0:T(8,128)}) custom-call(s32[2]{0:T(128)} %copy-done.26, f32[1,1]{1,0:T(1,128)} %bitcast.75.lr_ref, bf16[8,512,512]{2,1,0:T(8,128)(2,1)} %bitcast.126, f32[8,72,512]{2,1,0:T(8,128)} %bitcast.127, s32[8,1,512]{2,1,0:T(1,128)} %broadcast_in_dim.65.lab_ref, ...), custom_call_target="tpu_custom_call" | custom-call | flops 140000002048 | bytes 70000000 | tf_op jit(solution)/shard_map/head_dw/pallas_call | solution.py:597
  581.2 5.2 sort.15
  587.2 2.1 convert_element_type.139
  592.0 1.7 small_upd.1
  594.2 58.9 %all-gather.27.cloned.1.call-done = bf16[10240,512]{1,0:T(8,128)(2,1)} async-done(((bf16[1280,512]{1,0:T(8,128)(2,1)}), bf16[10240,512]{1,0:T(8,128)(2,1)}) %all-gather.27.cloned.1.call-update) | async-done | bytes 10485776 | tf_op jit(solution)/shard_map/all_gather | solution.py:938
  653.1 66.6 %expert_dw.2 = (f32[2,16,800,256]{3,2,1,0:T(8,128)}, f32[2,16,800,256]{3,2,1,0:T(8,128)}, f32[2,16,400,512]{3,2,1,0:T(8,128)}) custom-call(s32[8,17]{1,0:T(8,128)} %bitcast.122, s32[2]{0:T(128)} %copy-done.26, f32[1,1]{1,0:T(1,128)} %bitcast.76.lr_ref, bf16[8,1280,512]{2,1,0:T(8,128)(2,1)} %bitcast.125, f32[8,1280,512]{2,1,0:T(8,128)} %bitcast.124, ...), custom_call_target="tpu_custom_call" | custom-call | flops 60000002048 | bytes 150000000 | tf_op jit(solution)/shard_map/expert_dw/pallas_call | solution.py:441
  719.8 96.5 %all-gather.25.cloned.1.call-done = f32[10240,512]{1,0:T(8,128)} async-done(((f32[1280,512]{1,0:T(8,128)}), f32[10240,512]{1,0:T(8,128)}) %all-gather.25.cloned.1.call-update) | async-done | bytes 20971536 | tf_op jit(solution)/shard_map/all_gather | solution.py:951
  816.3 67.4 %expert_dw.3 = (f32[2,16,800,256]{3,2,1,0:T(8,128)}, f32[2,16,800,256]{3,2,1,0:T(8,128)}, f32[2,16,400,512]{3,2,1,0:T(8,128)}) custom-call(s32[8,17]{1,0:T(8,128)} %bitcast.118, s32[2]{0:T(128)} %copy-done.26, f32[1,1]{1,0:T(1,128)} %bitcast.77.lr_ref, ...), custom_call_target="tpu_custom_call", output_to_operand_aliasing={{0}: (14, {}), {1}: (15, {}), {2}: (16, {})} | custom-call | flops 60000002048 | bytes 150000000 | tf_op jit(solution)/shard_map/expert_dw/pallas_call | solution.py:441
  883.8 17.5 %head_upd.1 = f32[32064,256]{1,0:T(8,128)} custom-call(s32[2]{0:T(128)S(1)} %copy-done.27, f32[1,1]{1,0:T(1,128)} %bitcast.80.lr_ref, f32[16032,256]{1,0:T(8,128)} %collective-permute-done.5.grad_ref, f32[32064,256]{1,0:T(8,128)} %bitcast.96, f32[32064,256]{1,0:T(8,128)} %get-tuple-element.96.prev_ref), custom_call_target="tpu_custom_call", output_to_operand_aliasing={{}: (4, {})} | custom-call | flops 15000000512 | bytes 50000000 | tf_op jit(solution)/shard_map/head_upd/pallas_call | solution.py:626
  901.2 38.2 %embed_upd.1 = f32[16032,512]{1,0:T(8,128)} custom-call(s32[13]{0:T(128)S(1)} %convert_reduce_fusion.bounds, s32[4096]{0:T(1024)S(1)} %get-tuple-element.66.keys, s32[4096]{0:T(1024)S(1)} %get-tuple-element.67.perm, f32[1,1]{1,0:T(1,128)} %bitcast.78.lr_ref, bf16[4096,512]{1,0:T(8,128)(2,1)S(1)} %copy-done.31, f32[16032,512]{1,0:T(8,128)} %m_ref.1), custom_call_target="tpu_custom_call" | custom-call | flops 24999999488 | bytes 66000000 | tf_op jit(solution)/shard_map/embed_upd/pallas_call | solution.py:662
  (217 shorter events, 30.9 us)
Async XLA Ops:
  8.0 47.3 %all-gather.17.cloned.1.call-start = ((), (), s32[]{:S(2)}) async-start(), calls=%async_computation.2 | async-start | bytes 1474560 | tf_op jit(solution)/shard_map/all_gather | solution.py:899
  8.9 117.5 %copy-start = (s32[1,1,512,2]{3,2,1,0:T(8,128)}, s32[1,1,512,2]{3,2,1,0:T(8,128)S(1)}, u32[]{:S(2)}) copy-start(s32[1,1,512,2]{3,2,1,0:T(8,128)S(1)} %copy.86) | copy-start | bytes 12292
  9.3 151.3 %copy-start.1 = (s32[1,1,512,2]{3,2,1,0:T(8,128)}, s32[1,1,512,2]{3,2,1,0:T(8,128)S(1)}, u32[]{:S(2)}) copy-start(s32[1,1,512,2]{3,2,1,0:T(8,128)S(1)} %copy.87) | copy-start | bytes 12292
  9.7 116.7 %copy-start.29 = (s32[17]{0:T(128)}, s32[17]{0:T(128)S(1)}, u32[]{:S(2)}) copy-start(s32[17]{0:T(128)S(1)} %select_reduce_fusion.3.off) | copy-start | bytes 208
  9.8 150.9 %copy-start.30 = (s32[17]{0:T(128)}, s32[17]{0:T(128)S(1)}, u32[]{:S(2)}) copy-start(s32[17]{0:T(128)S(1)} %select_reduce_fusion.2.off) | copy-start | bytes 208
  14.1 105.9 %all-gather.19.cloned.1.call-start = ((), (), s32[]{:S(2)}) async-start(), calls=%async_computation.3 | async-start | bytes 3932160 | tf_op jit(solution)/shard_map/all_gather | solution.py:913
  27.9 98.4 %collective-permute-start.1 = (bf16[2,16,800,256]{3,2,1,0:T(8,128)(2,1)}, bf16[2,16,800,256]{3,2,1,0:T(8,128)(2,1)}, u32[]{:S(2)}, u32[]{:S(2)}) collective-permute-start(bf16[2,16,800,256]{3,2,1,0:T(8,128)(2,1)} %convert_element_type.130.refs_0_), channel_id=1, source_target_pairs={{0,1},{1,0},{2,3},{3,2},{4,5},{5,4},{6,7},{7,6}} | collective-permute-start | bytes 39321608 | tf_op jit(solution)/shard_map/ppermute | solution.py:917
  40.9 85.5 %collective-permute-start.2 = (bf16[2,16,800,256]{3,2,1,0:T(8,128)(2,1)}, bf16[2,16,800,256]{3,2,1,0:T(8,128)(2,1)}, u32[]{:S(2)}, u32[]{:S(2)}) collective-permute-start(bf16[2,16,800,256]{3,2,1,0:T(8,128)(2,1)} %convert_element_type.131.refs_2_), channel_id=1, source_target_pairs={{0,1},{1,0},{2,3},{3,2},{4,5},{5,4},{6,7},{7,6}} | collective-permute-start | bytes 39321608 | tf_op jit(solution)/shard_map/ppermute | solution.py:917
  55.3 71.1 %collective-permute-start.3 = (bf16[2,16,400,512]{3,2,1,0:T(8,128)(2,1)}, bf16[2,16,400,512]{3,2,1,0:T(8,128)(2,1)}, u32[]{:S(2)}, u32[]{:S(2)}) collective-permute-start(bf16[2,16,400,512]{3,2,1,0:T(8,128)(2,1)} %convert_element_type.132.refs_4_), channel_id=1, source_target_pairs={{0,1},{1,0},{2,3},{3,2},{4,5},{5,4},{6,7},{7,6}} | collective-permute-start | bytes 39321608 | tf_op jit(solution)/shard_map/ppermute | solution.py:917
  91.2 101.1 %collective-permute-start.4 = (bf16[32064,256]{1,0:T(8,128)(2,1)}, bf16[32064,256]{1,0:T(8,128)(2,1)}, u32[]{:S(2)}, u32[]{:S(2)}) collective-permute-start(bf16[32064,256]{1,0:T(8,128)(2,1)} %convert_element_type.138.wa_ref), channel_id=1, source_target_pairs={{0,1},{1,0},{2,3},{3,2},{4,5},{5,4},{6,7},{7,6}} | collective-permute-start | bytes 49250312 | tf_op jit(solution)/shard_map/ppermute | solution.py:917
  93.1 276.9 %reduce-scatter.3.cloned.1.call-start = ((), (), s32[]{:S(2)}) async-start(), calls=%async_computation.4 | async-start | bytes 4055040 | tf_op jit(solution)/shard_map/reduce_scatter | solution.py:953
  98.1 20.7 %collective-permute-start = (bf16[512,512]{1,0:T(8,128)(2,1)}, bf16[512,512]{1,0:T(8,128)(2,1)S(1)}, u32[]{:S(2)}, u32[]{:S(2)}) collective-permute-start(bf16[512,512]{1,0:T(8,128)(2,1)} %slice.133), channel_id=1, source_target_pairs={{0,1},{1,0},{2,3},{3,2},{4,5},{5,4},{6,7},{7,6}} | collective-permute-start | bytes 1572872 | tf_op jit(solution)/shard_map/ppermute | solution.py:924
  360.1 21.6 %reduce-scatter.5.cloned.1.call-start = ((), (), s32[]{:S(2)}) async-start(), calls=%async_computation.5 | async-start | bytes 4055040 | tf_op jit(solution)/shard_map/reduce_scatter | solution.py:953
  360.7 35.9 %all-gather.31.cloned.1.call-start = ((), (), s32[]{:S(2)}) async-start(), calls=%async_computation.11 | async-start | bytes 4718592 | tf_op jit(solution)/shard_map/all_gather | solution.py:942
  361.4 55.3 %all-gather.33.cloned.1.call-start = ((), (), s32[]{:S(2)}) async-start(), calls=%async_computation.12 | async-start | bytes 1327104 | tf_op jit(solution)/shard_map/all_gather | solution.py:943
  362.2 227.1 %all-reduce.4.cloned.1.call-start = ((), (), s32[]{:S(2)}) async-start(), calls=%async_computation.13 | async-start | bytes 5406720 | tf_op jit(solution)/shard_map/psum | solution.py:953
  381.7 212.5 %all-gather.29.cloned.1.call-start = ((), (), s32[]{:S(2)}) async-start(), calls=%async_computation.10 | async-start | bytes 23592960 | tf_op jit(solution)/shard_map/all_gather | solution.py:951
  382.3 270.8 %all-gather.27.cloned.1.call-start = ((), (), s32[]{:S(2)}) async-start(), calls=%async_computation.9 | async-start | bytes 11796480 | tf_op jit(solution)/shard_map/all_gather | solution.py:938
  382.9 336.9 %all-gather.23.cloned.1.call-start = ((), (), s32[]{:S(2)}) async-start(), calls=%async_computation.7 | async-start | bytes 11796480 | tf_op jit(solution)/shard_map/all_gather | solution.py:938
  383.6 432.6 %all-gather.25.cloned.1.call-start = ((), (), s32[]{:S(2)}) async-start(), calls=%async_computation.8 | async-start | bytes 23592960 | tf_op jit(solution)/shard_map/all_gather | solution.py:951
  384.4 499.4 %all-gather.21.cloned.1.call-start = ((), (), s32[]{:S(2)}) async-start(), calls=%async_computation.6 | async-start | bytes 4718592 | tf_op jit(solution)/shard_map/all_gather | solution.py:955
  416.8 164.3 %slice-start = ((s32[8,1058]{1,0:T(8,128)}), s32[8,34]{1,0:T(8,128)S(1)}, s32[]{:S(2)}) async-start(s32[8,1058]{1,0:T(8,128)} %copy-done.47), calls=%async_computation.14 | async-start | bytes 8192 | tf_op jit(solution)/shard_map/slice | solution.py:910
  416.8 164.4 %copy-start.48 = (s32[1,4,8,128]{3,2,1,0:T(8,128)S(1)}, s32[1,4,8,128]{3,2,1,0:T(8,128)}, u32[]{:S(2)}) copy-start(s32[1,4,8,128]{3,2,1,0:T(8,128)} %get-tuple-element.136) | copy-start | bytes 49156
  416.8 172.5 %copy-start.3 = (f32[2,256,512]{2,1,0:T(8,128)S(1)}, f32[2,256,512]{2,1,0:T(8,128)}, u32[]{:S(2)}) copy-start(f32[2,256,512]{2,1,0:T(8,128)} %refs_5_.1) | copy-start | bytes 3145732
  416.8 172.5 %copy-start.5 = (f32[2,256,512]{2,1,0:T(8,128)S(1)}, f32[2,256,512]{2,1,0:T(8,128)}, u32[]{:S(2)}) copy-start(f32[2,256,512]{2,1,0:T(8,128)} %refs_2_.1) | copy-start | bytes 3145732
  416.8 172.6 %copy-start.8 = (f32[2,256,128]{2,1,0:T(8,128)S(1)}, f32[2,256,128]{2,1,0:T(8,128)}, u32[]{:S(2)}) copy-start(f32[2,256,128]{2,1,0:T(8,128)} %refs_4_.1) | copy-start | bytes 786436
  416.8 172.6 %copy-start.10 = (f32[2,256,128]{2,1,0:T(8,128)S(1)}, f32[2,256,128]{2,1,0:T(8,128)}, u32[]{:S(2)}) copy-start(f32[2,256,128]{2,1,0:T(8,128)} %refs_3_.1) | copy-start | bytes 786436
  416.8 172.6 %copy-start.15 = (f32[2,256,16]{1,2,0:T(8,128)S(1)}, f32[2,256,16]{1,2,0:T(8,128)}, u32[]{:S(2)}) copy-start(f32[2,256,16]{1,2,0:T(8,128)} %param.30) | copy-start | bytes 98308
  416.8 172.6 %copy-start.24 = (f32[2,256]{1,0:T(2,128)S(1)}, f32[2,256]{1,0:T(2,128)}, u32[]{:S(2)}) copy-start(f32[2,256]{1,0:T(2,128)} %refs_8_.5) | copy-start | bytes 6148
  416.8 172.5 %copy-start.25 = (f32[2,256]{1,0:T(2,128)S(1)}, f32[2,256]{1,0:T(2,128)}, u32[]{:S(2)}) copy-start(f32[2,256]{1,0:T(2,128)} %refs_7_.1) | copy-start | bytes 6148
  416.8 172.5 %copy-start.28 = (f32[256]{0:T(256)S(1)}, f32[256]{0:T(256)}, u32[]{:S(2)}) copy-start(f32[256]{0:T(256)} %param.34) | copy-start | bytes 3076
  580.8 302.9 %collective-permute-start.5 = (f32[16032,256]{1,0:T(8,128)}, f32[16032,256]{1,0:T(8,128)}, u32[]{:S(2)}, u32[]{:S(2)}) collective-permute-start(f32[16032,256]{1,0:T(8,128)} %get-tuple-element.115), channel_id=1, source_target_pairs={{0,1},{1,0},{2,3},{3,2},{4,5},{5,4},{6,7},{7,6}} | collective-permute-start | bytes 49250312 | tf_op jit(solution)/shard_map/ppermute | solution.py:959
  (39 other events, 1054.0 us)
Sparse Core Ops, SparseCore 0:
  14.3 21.7 all-gather.16
  363.3 33.2 all-gather.30
  398.4 18.3 all-gather.32
  419.8 68.7 all-reduce.3
  490.3 103.4 all-gather.28
  595.5 57.5 all-gather.26
  654.9 57.5 all-gather.22
  714.3 101.8 all-gather.24
  818.1 31.0 all-gather.20
Sparse Core Ops, SparseCore 1:
  93.2 12.0 all-gather.18
  360.2 9.8 reduce-scatter.2
  372.7 8.9 reduce-scatter.4
